TPU v7x, 64 devices: a 2x2x8 block of a 4x4x8 slice. The times are simulated.
64 devices in a mesh: dp: 4 (over x, y), tp: 16 (over z, core).
Axes of the slice: x: 2, y: 2, z: 8, core: 2. Of those that a mesh axis runs over, the one named last changes fastest.
The devices are a block of a 4x4x8 slice.
Arguments:
- hidden: bfloat16 [2048, 4096], P('dp'), parts along dimension 0
- w_q: bfloat16 [4096, 4096], P(None, 'tp')
- w_k: bfloat16 [4096, 4096], P(None, 'tp')
- w_v: bfloat16 [4096, 4096], P(None, 'tp')
- w_o: bfloat16 [4096, 4096], P('tp')
- q_norm_w: float32 [4096], P('tp')
- k_norm_w: float32 [4096], P('tp')
- post_norm_w: float32 [4096], replicated
- k_cache: bfloat16 [2048, 16, 32, 128], P('dp', None, 'tp'), parts along dimension 0
- v_cache: bfloat16 [2048, 16, 32, 128], P('dp', None, 'tp'), parts along dimension 0
- positions: int32 [2048], P('dp'), parts along dimension 0
Outputs:
- output 1: bfloat16 [2048, 4096], P('dp'), parts along dimension 0
- output 2: bfloat16 [2048, 16, 32, 128], P('dp', None, 'tp'), parts along dimension 0
- output 3: bfloat16 [2048, 16, 32, 128], P('dp', None, 'tp'), parts along dimension 0
There are 4 independent parts. A program takes and returns all parts, laid end to end along the dimension named above; an argument that names none is the same for every part.
All inputs are finite; a program needn't handle non-finite values.
Results may differ from a plain program's by a relative error of at most 0.0138914.
Values are sent between devices in bfloat16 or wider.
A program may use at most 768 MiB of HBM per device.

v0:
```python
import jax
import jax.numpy as jnp
from jax import lax
from jax.sharding import PartitionSpec as P

NORM_EPS = 1e-6
ROPE_BASE = 500000.0


def apply_rope(heads_val, positions):
    head_dim = heads_val.shape[-1]
    half = head_dim // 2
    inv_freq = ROPE_BASE ** (-2.0 * jnp.arange(half, dtype=jnp.float32) / head_dim)
    angles = positions.astype(jnp.float32)[:, None, None] * inv_freq[None, None, :]
    cos_tab = jnp.cos(angles)
    sin_tab = jnp.sin(angles)
    wide = heads_val.astype(jnp.float32)
    first = wide[..., :half]
    second = wide[..., half:]
    return jnp.concatenate([first * cos_tab - second * sin_tab, second * cos_tab + first * sin_tab], axis=-1).astype(jnp.bfloat16)


def write_slot(cache, new_vals, positions):
    slot_ids = jnp.arange(cache.shape[1], dtype=jnp.int32)
    at_slot = (slot_ids[None, :] == positions[:, None])[:, :, None, None]
    return jnp.where(at_slot, new_vals[:, None], cache)


def attend(q_rot, k_new, v_new, positions):
    slot_ids = jnp.arange(k_new.shape[1], dtype=jnp.int32)
    scores = jnp.einsum('bhd,bshd->bhs', q_rot, k_new, preferred_element_type=jnp.float32) * k_new.shape[3] ** -0.5
    valid = (slot_ids[None, :] <= positions[:, None])[:, None, :]
    scores = jnp.where(valid, scores, -1e30)
    probs = jax.nn.softmax(scores, axis=-1).astype(jnp.bfloat16)
    return jnp.einsum('bhs,bshd->bhd', probs, v_new, preferred_element_type=jnp.float32).astype(jnp.bfloat16)


def solution(mesh):
    def local_step(hidden, w_q, w_k, w_v, w_o, q_norm_w, k_norm_w, post_norm_w, k_cache, v_cache, positions):
        n_rows, width = hidden.shape
        local_heads, head_dim = k_cache.shape[2], k_cache.shape[3]
        q_local = jnp.dot(hidden, w_q, preferred_element_type=jnp.float32).astype(jnp.bfloat16).astype(jnp.float32)
        k_local = jnp.dot(hidden, w_k, preferred_element_type=jnp.float32).astype(jnp.bfloat16).astype(jnp.float32)
        v_local = jnp.dot(hidden, w_v, preferred_element_type=jnp.float32).astype(jnp.bfloat16)
        energy = jnp.stack([jnp.sum(q_local * q_local, axis=-1), jnp.sum(k_local * k_local, axis=-1)])
        energy = lax.psum(energy, 'tp')
        inv_rms = lax.rsqrt(energy / width + NORM_EPS)
        q_normed = (q_local * inv_rms[0][:, None] * q_norm_w).astype(jnp.bfloat16).reshape(n_rows, local_heads, head_dim)
        k_normed = (k_local * inv_rms[1][:, None] * k_norm_w).astype(jnp.bfloat16).reshape(n_rows, local_heads, head_dim)
        q_rot = apply_rope(q_normed, positions)
        k_rot = apply_rope(k_normed, positions)
        k_new = write_slot(k_cache, k_rot, positions)
        v_new = write_slot(v_cache, v_local.reshape(n_rows, local_heads, head_dim), positions)
        attn = attend(q_rot, k_new, v_new, positions)
        proj_part = jnp.dot(attn.reshape(n_rows, local_heads * head_dim), w_o, preferred_element_type=jnp.float32).astype(jnp.bfloat16)
        a_out = lax.psum(proj_part, 'tp').astype(jnp.float32)
        inv_out = lax.rsqrt(jnp.mean(a_out * a_out, axis=-1, keepdims=True) + NORM_EPS)
        hidden_out = (hidden.astype(jnp.float32) + a_out * inv_out * post_norm_w).astype(jnp.bfloat16)
        return hidden_out, k_new, v_new

    cache_spec = P('dp', None, 'tp', None)
    return jax.shard_map(local_step, mesh=mesh, in_specs=(P('dp', None), P(None, 'tp'), P(None, 'tp'), P(None, 'tp'), P('tp', None), P('tp'), P('tp'), P(None), cache_spec, cache_spec, P('dp')), out_specs=(P('dp', None), cache_spec, cache_spec), check_vma=False)
```

profile of v0, /device:TPU:21, one launch (start us, length us, event | category | flops | bytes accessed | tf_op | source)
XLA Modules:
  0.0 230.8 jit_solution(13343658920327957031)
XLA Ops:
  7.2 0.0 copy-start
  7.2 0.1 all-reduce.2.cloned.1.call-start
  7.3 0.8 convert_element_type.69
  8.1 0.8 iota_compare_fusion.1
  8.9 0.1 copy.16
  9.0 4.2 %convolution_convert_fusion.1 = bf16[512,256]{0,1:T(8,128)(2,1)S(1)} fusion(bf16[512,4096]{1,0:T(8,128)(2,1)} %param.11, bf16[4096,256]{1,0:T(8,128)(2,1)} %param.14), kind=kOutput, calls=%fused_computation.14 | convolution fusion | flops 1073872896 | bytes 6553600 | tf_op jit(solution)/shard_map/dot_general | solution.py:44
  13.2 0.2 copy.18
  13.4 0.0 copy-start.3
  13.4 0.0 copy-start.7
  13.4 4.3 %multiply_reduce_fusion.2 = (f32[512]{0:T(512)S(1)}, f32[512,256]{0,1:T(8,128)S(1)}) fusion(bf16[512,4096]{1,0:T(8,128)(2,1)} %param.11, bf16[4096,256]{1,0:T(8,128)(2,1)} %param.12), kind=kOutput, calls=%fused_computation.27 | convolution fusion | flops 1074265600 | bytes 6817792 | tf_op jit(solution)/shard_map/dot_general | solution.py:42
  17.7 0.0 copy-done.3
  17.7 0.4 copy-done.7
  18.1 0.0 copy-start.5
  18.1 0.0 copy-start.6
  18.1 1.3 multiply_reduce_fusion.1
  19.5 29.0 %psum.14 = f32[2,512]{1,0:T(2,128)S(1)} all-reduce(f32[2,512]{1,0:T(2,128)S(1)} %pad_maximum_fusion.1), channel_id=1, replica_groups=mesh['dp'=4,'tp'=16] {'tp'}, use_global_device_ids=true, to_apply=%region_2.0 | all-reduce | flops 1024 | bytes 8192 | tf_op jit(solution)/shard_map/psum | solution.py:46
  48.5 0.0 copy-done.5
  48.5 0.1 multiply_convert_fusion.1
  48.6 0.1 convert.20
  48.7 0.0 copy-done.6
  48.7 0.1 multiply_convert_fusion
  48.8 0.1 convert.21
  48.8 0.5 multiply_cosine_fusion
  49.4 0.2 subtract_convert_fusion
  49.6 0.8 maximum_convert_fusion
  50.3 0.2 copy.29
  50.6 1.1 copy.17
  51.7 26.0 %multiply_reduce_fusion = (f32[512,2,16]{1,2,0:T(8,128)}, bf16[512,16,2,128]{3,2,1,0:T(2,128)(2,1)}) fusion(f32[512,2,128]{2,1,0:T(2,128)S(1)} %copy.29, bf16[512,16,2,128]{3,2,1,0:T(2,128)(2,1)} %param.19, bf16[512,2,128]{2,1,0:T(2,128)(2,1)S(1)} %copy.17, pred[512,16]{1,0:T(8,128)(4,1)S(1)} %get-tuple-element.16), kind=kLoop, calls=%fused_computation.8 | loop fusion | flops 8372224 | bytes 9248768
  77.7 2.8 %copy.25 = f32[512,2,16]{0,2,1:T(8,128)S(1)} copy(f32[512,2,16]{1,2,0:T(8,128)} %get-tuple-element.3) | data formatting | bytes 131072 | tf_op jit(solution)/shard_map/bhd,bshd->bhs/dot_general | solution.py:31
  80.6 0.4 copy.26
  81.0 12.3 %broadcast_select_fusion = bf16[512,16,2,128]{3,2,1,0:T(2,128)(2,1)S(1)} fusion(bf16[512,16,2,128]{3,2,1,0:T(2,128)(2,1)} %param.20, pred[512,16]{1,0:T(8,128)(4,1)S(1)} %get-tuple-element.16, bf16[512,2,128]{2,1,0:T(2,128)(2,1)S(1)} %copy.18), kind=kLoop, calls=%fused_computation.9 | loop fusion | flops 2097152 | bytes 8658944 | tf_op jit(solution)/shard_map/jit(_where)/select_n | solution.py:26
  93.3 0.0 copy-start.2
  93.4 2.0 copy-done.2
  95.4 1.2 fusion.6
  96.6 0.2 convert_element_type.75
  96.8 0.0 copy-done
  96.8 3.3 %convolution_convert_fusion = bf16[512,4096]{1,0:T(8,128)(2,1)} fusion(bf16[256,4096]{1,0:T(8,128)(2,1)S(1)} %copy-done, bf16[64,8,2,128]{3,2,1,0:T(2,128)(2,1)S(1)} %bitcast.27), kind=kOutput, calls=%fused_computation.11 | convolution fusion | flops 1075838976 | bytes 6553600 | tf_op jit(solution)/shard_map/dot_general | solution.py:55
  100.1 0.0 copy-start.4
  100.1 0.1 all-reduce.2.cloned.1.call-update
  100.1 114.0 %all-reduce.2.cloned.1.call-done = bf16[512,4096]{1,0:T(8,128)(2,1)} async-done(((bf16[512,4096]{1,0:T(8,128)(2,1)}), bf16[512,4096]{1,0:T(8,128)(2,1)}) %all-reduce.2.cloned.1.call-update) | async-done | bytes 4194320 | tf_op jit(solution)/shard_map/psum | solution.py:56
  214.2 0.0 copy-start.1
  214.2 3.2 %fusion.2 = f32[512]{0:T(512)S(1)} fusion(bf16[512,4096]{1,0:T(8,128)(2,1)} %all-reduce.2.cloned.1.call-done), kind=kLoop, calls=%fused_computation.4 | loop fusion | flops 6290944 | bytes 4196352 | tf_op jit(solution)/shard_map/reduce_sum | solution.py:57
  217.4 0.0 copy-done.4
  217.4 0.2 copy-done.1
  217.6 6.4 %fusion.5 = bf16[512,4096]{1,0:T(8,128)(2,1)} fusion(bf16[512,4096]{1,0:T(8,128)(2,1)S(1)} %copy-done.1, bf16[512,4096]{1,0:T(8,128)(2,1)} %param.11, f32[4096]{0:T(1024)S(1)} %copy-done.4, f32[512]{0:T(512)S(1)} %add_rsqrt_fusion.1), kind=kLoop, calls=%fused_computation.7 | loop fusion | flops 12582912 | bytes 12601344 | tf_op jit(solution)/shard_map/convert_element_type | solution.py:58
  (6 shorter events, 0.1 us)
Async XLA Ops:
  7.2 89.6 %copy-start = (bf16[256,4096]{1,0:T(8,128)(2,1)S(1)}, bf16[256,4096]{1,0:T(8,128)(2,1)}, u32[]{:S(2)}) copy-start(bf16[256,4096]{1,0:T(8,128)(2,1)} %param.15) | copy-start | bytes 6291460
  7.2 207.0 %all-reduce.2.cloned.1.call-start = ((), (), s32[]{:S(2)}) async-start(), calls=%async_computation | async-start | bytes 8388608 | tf_op jit(solution)/shard_map/psum | solution.py:56
  13.4 4.3 %copy-start.3 = (bf16[512,4096]{1,0:T(8,128)(2,1)S(1)}, bf16[512,4096]{1,0:T(8,128)(2,1)}, u32[]{:S(2)}) copy-start(bf16[512,4096]{1,0:T(8,128)(2,1)} %param.11) | copy-start | bytes 12582916
  13.4 4.7 %copy-start.7 = (bf16[4096,256]{1,0:T(8,128)(2,1)S(1)}, bf16[4096,256]{1,0:T(8,128)(2,1)}, u32[]{:S(2)}) copy-start(bf16[4096,256]{1,0:T(8,128)(2,1)} %param.13) | copy-start | bytes 6291460
  18.1 30.4 %copy-start.5 = (f32[256]{0:T(256)S(1)}, f32[256]{0:T(256)}, u32[]{:S(2)}) copy-start(f32[256]{0:T(256)} %param.16) | copy-start | bytes 3076
  18.1 30.5 %copy-start.6 = (f32[256]{0:T(256)S(1)}, f32[256]{0:T(256)}, u32[]{:S(2)}) copy-start(f32[256]{0:T(256)} %param.17) | copy-start | bytes 3076
  93.3 2.0 copy-start.2
  100.1 117.3 %copy-start.4 = (f32[4096]{0:T(1024)S(1)}, f32[4096]{0:T(1024)}, u32[]{:S(2)}) copy-start(f32[4096]{0:T(1024)} %param.18) | copy-start | bytes 49156
  214.2 3.4 %copy-start.1 = (bf16[512,4096]{1,0:T(8,128)(2,1)S(1)}, bf16[512,4096]{1,0:T(8,128)(2,1)}, u32[]{:S(2)}) copy-start(bf16[512,4096]{1,0:T(8,128)(2,1)} %all-reduce.2.cloned.1.call-done) | copy-start | bytes 12582916
Sparse Core Ops, SparseCore 0:
  100.3 113.8 all-reduce.1
where the time goes:
time: 231 us
  waiting for transfers between devices  114 us (49%)
  other arithmetic  51.6 us (22%)
  blocking collectives  29 us (13%)
  matrix products  14.3 us (6%)
  between operations  14.3 us (6%)
  local copies, waits for them, and re-layouts  7.48 us (3%)
    psum x1, waiting for transfers between devices, local_step(): a_out = lax.psum(proj_part, 'tp').astype(jnp.float32)  114 us
    psum x1, blocking collectives, local_step(): energy = lax.psum(energy, 'tp')  29 us
    unnamed x2, other arithmetic  26.8 us
    select_n x1, other arithmetic, write_slot(): return jnp.where(at_slot, new_vals[:, None], cache)  12.3 us
    convert_element_type x1, other arithmetic, local_step(): (hidden.astype(jnp.float32) + a_out * inv_out * post_norm_w).astype(jnp.b...  6.36 us
  transfers between devices with their start and end apart: 1, of which 1 were waited for; matrix products, arithmetic and copies ran while one was open for 0% of the time, Pallas kernels for 0%

commit v1 on v0

--- a/solution.py
+++ b/solution.py
@@ -1,10 +1,15 @@
+import functools
+
 import jax
 import jax.numpy as jnp
 from jax import lax
+from jax.experimental import pallas as pl
+from jax.experimental.pallas import tpu as pltpu
 from jax.sharding import PartitionSpec as P
 
 NORM_EPS = 1e-6
 ROPE_BASE = 500000.0
+OUT_VMEM = True
 
 
 def apply_rope(heads_val, positions):
@@ -33,6 +38,222 @@
     scores = jnp.where(valid, scores, -1e30)
     probs = jax.nn.softmax(scores, axis=-1).astype(jnp.bfloat16)
     return jnp.einsum('bhs,bshd->bhd', probs, v_new, preferred_element_type=jnp.float32).astype(jnp.bfloat16)
+
+
+MESH = pl.DeviceIdType.MESH
+SUBS = 2
+LAG = 2
+
+
+def finish_kernel(n_tp, o_ref, w_ref, hid_ref, gain_ref, out_ref,
+                  o_in, w_in, hid, share, rs_in, rs_out,
+                  x_send, x_recv, h_sem, rs_send, rs_recv, ag_send, ag_recv, d2d_send, d2d_recv):
+    nz = n_tp // 2
+    t = lax.axis_index("tp")
+    z, k = t // 2, lax.rem(t, 2)
+    up, down, mate = lax.rem(t + 2, n_tp), lax.rem(t + n_tp - 2, n_tp), z * 2 + 1 - k
+    n_rows, width = out_ref.shape
+    half_rows = n_rows // 2
+    rows = half_rows // nz
+    sub = rows // SUBS
+    half = width // 2
+    far = nz // 2
+    chunk_of = lambda j: lax.rem(z + nz + j, nz)
+    out_row = lambda j, s: pl.multiple_of(k * half_rows + chunk_of(j) * rows + s * sub, sub)
+    cols = (pl.ds(0, half), pl.ds(half, half))
+    target = (up, down)
+    long_half = (0, 1)
+
+    barrier = pltpu.get_barrier_semaphore()
+    for peer in (up, down, mate):
+        pl.semaphore_signal(barrier, inc=1, device_id={"tp": peer}, device_id_type=MESH)
+    hid_copy = pltpu.make_async_copy(hid_ref.at[pl.ds(pl.multiple_of(k * half_rows + z * rows, rows), rows), :], hid, h_sem)
+    hid_copy.start()
+    pl.semaphore_wait(barrier, 3)
+
+    o_copy = pltpu.make_async_remote_copy(
+        o_ref.at[pl.ds(pl.multiple_of((1 - k) * half_rows, half_rows), half_rows), :], o_in,
+        x_send.at[0], x_recv.at[0], device_id={"tp": mate}, device_id_type=MESH)
+    w_copy = pltpu.make_async_remote_copy(w_ref, w_in, x_send.at[1], x_recv.at[1], device_id={"tp": mate}, device_id_type=MESH)
+    o_copy.start()
+    w_copy.start()
+    o_copy.wait_recv()
+    w_copy.wait_recv()
+
+    tile = min(1024, width)
+
+    def make_share(j):
+        own = o_ref[pl.ds(pl.multiple_of(k * half_rows + chunk_of(j) * rows, rows), rows), :]
+        other = o_in[pl.ds(pl.multiple_of(chunk_of(j) * rows, rows), rows), :]
+
+        def one(c, carry):
+            at = pl.ds(pl.multiple_of(c * tile, tile), tile)
+            share[j % nz, :, at] = (jnp.dot(own, w_ref[:, at], preferred_element_type=jnp.float32)
+                                    + jnp.dot(other, w_in[:, at], preferred_element_type=jnp.float32))
+            return carry
+
+        lax.fori_loop(0, width // tile, one, 0)
+
+    def hops(d, c):
+        return far if c == long_half[d] else far - 1
+
+    slots = {}
+    for d in range(2):
+        for c in range(2):
+            for h in range(hops(d, c)):
+                for s in range(SUBS):
+                    slots[d, c, h, s] = len(slots)
+
+    def rs_message(d, c, h, s):
+        i = slots[d, c, h, s]
+        return pltpu.make_async_remote_copy(
+            rs_out.at[i], rs_in.at[i], rs_send.at[i], rs_recv.at[i], device_id={"tp": target[d]}, device_id_type=MESH)
+
+    def piece(j, c, s):
+        return share[j % nz, s * sub:(s + 1) * sub, c * half:(c + 1) * half]
+
+    def rs_step(d, c, h, s):
+        ahead = hops(d, c) - h
+        j = ahead if d == 0 else -ahead
+        value = piece(j, c, s)
+        if h > 0:
+            before = rs_message(d, c, h - 1, s)
+            before.wait_recv()
+            value = value + rs_in[slots[d, c, h - 1, s]].astype(jnp.float32)
+        rs_out[slots[d, c, h, s]] = value.astype(jnp.bfloat16)
+        rs_message(d, c, h, s).start()
+
+    def ag_message(d, c, h, s):
+        j = -h if d == 0 else h
+        here = out_ref.at[pl.ds(out_row(j, s), sub), cols[c]]
+        i = slots[d, c, h, s]
+        return pltpu.make_async_remote_copy(
+            here, here, ag_send.at[i], ag_recv.at[i], device_id={"tp": target[d]}, device_id_type=MESH)
+
+    def ag_arrival(d, c, h, s):
+        j = -(h + 1) if d == 0 else h + 1
+        here = out_ref.at[pl.ds(out_row(j, s), sub), cols[c]]
+        i = slots[d, c, h, s]
+        return pltpu.make_async_remote_copy(
+            here, here, ag_send.at[i], ag_recv.at[i], device_id={"tp": target[d]}, device_id_type=MESH)
+
+    d2d = []
+
+    def d2d_start(j, c, s):
+        here = out_ref.at[pl.ds(out_row(j, s), sub), cols[c]]
+        i = len(d2d)
+        copy = pltpu.make_async_remote_copy(here, here, d2d_send.at[i], d2d_recv.at[i], device_id={"tp": mate}, device_id_type=MESH)
+        copy.start()
+        d2d.append((j, c, s))
+
+    def finish(s):
+        total = []
+        for c in range(2):
+            acc = piece(0, c, s)
+            for d in range(2):
+                last = hops(d, c) - 1
+                rs_message(d, c, last, s).wait_recv()
+                acc = acc + rs_in[slots[d, c, last, s]].astype(jnp.float32)
+            share[0, s * sub:(s + 1) * sub, c * half:(c + 1) * half] = acc
+            total.append(jnp.sum(acc * acc, axis=-1, keepdims=True))
+        inv = lax.rsqrt((total[0] + total[1]) / width + NORM_EPS)
+        for c in range(2):
+            at = slice(c * half, (c + 1) * half)
+            normed = share[0, s * sub:(s + 1) * sub, at] * inv * gain_ref[:, at]
+            out_ref[pl.ds(out_row(0, s), sub), at] = (hid[s * sub:(s + 1) * sub, at].astype(jnp.float32) + normed).astype(jnp.bfloat16)
+        for d in range(2):
+            for c in (long_half[d], 1 - long_half[d]):
+                ag_message(d, c, 0, s).start()
+        for c in range(2):
+            d2d_start(0, c, s)
+
+    def ag_step(h, s):
+        for c in range(2):
+            for d in range(2):
+                if h - 1 < hops(d, c):
+                    ag_arrival(d, c, h - 1, s).wait_recv()
+                    if h < hops(d, c):
+                        ag_message(d, c, h, s).start()
+                    d2d_start(-h if d == 0 else h, c, s)
+
+    def stage(g, s):
+        if g < far:
+            for longer in (True, False):
+                for d in range(2):
+                    c = long_half[d] if longer else 1 - long_half[d]
+                    if g < hops(d, c):
+                        if g == 0 and s == 0:
+                            j = hops(d, c) if d == 0 else -hops(d, c)
+                            if j % nz not in made:
+                                make_share(j)
+                                made.add(j % nz)
+                        rs_step(d, c, g, s)
+            if g == 0 and s == 0:
+                for j in sorted(range(nz), key=lambda j: -min(j, nz - j)):
+                    if j not in made:
+                        make_share(j)
+                        made.add(j)
+        elif g == far:
+            if s == 0:
+                hid_copy.wait()
+            finish(s)
+        else:
+            ag_step(g - far, s)
+
+    made = set()
+    last_stage = 2 * far
+    for slot in range(last_stage + 1 + LAG * (SUBS - 1)):
+        for s in range(SUBS):
+            g = slot - LAG * s
+            if 0 <= g <= last_stage:
+                stage(g, s)
+
+    o_copy.wait_send()
+    w_copy.wait_send()
+    for (d, c, h, s) in slots:
+        rs_message(d, c, h, s).wait_send()
+        ag_message(d, c, h, s).wait_send()
+    for i, (j, c, s) in enumerate(d2d):
+        here = out_ref.at[pl.ds(out_row(j, s), sub), cols[c]]
+        there = out_ref.at[pl.ds(pl.multiple_of((1 - k) * half_rows + chunk_of(j) * rows + s * sub, sub), sub), cols[c]]
+        copy = pltpu.make_async_remote_copy(here, there, d2d_send.at[i], d2d_recv.at[i], device_id={"tp": mate}, device_id_type=MESH)
+        copy.wait_send()
+        copy.wait_recv()
+
+
+def finish_call(n_tp, attn, w_o, hidden, gain):
+    n_rows, width = hidden.shape
+    depth = w_o.shape[0]
+    nz = n_tp // 2
+    half_rows, rows = n_rows // 2, n_rows // n_tp
+    sub = rows // SUBS
+    n_msg = 2 * SUBS * (nz - 1)
+    vmem = pl.BlockSpec(memory_space=pltpu.VMEM)
+    return pl.pallas_call(
+        functools.partial(finish_kernel, n_tp),
+        name="finish",
+        out_shape=pltpu.VMEM((n_rows, width), jnp.bfloat16) if OUT_VMEM else jax.ShapeDtypeStruct((n_rows, width), jnp.bfloat16),
+        in_specs=[vmem, vmem, pl.BlockSpec(memory_space=pl.ANY), vmem],
+        out_specs=vmem,
+        scratch_shapes=[
+            pltpu.VMEM((half_rows, depth), jnp.bfloat16),
+            pltpu.VMEM((depth, width), jnp.bfloat16),
+            pltpu.VMEM((rows, width), jnp.bfloat16),
+            pltpu.VMEM((nz, rows, width), jnp.float32),
+            pltpu.VMEM((n_msg, sub, width // 2), jnp.bfloat16),
+            pltpu.VMEM((n_msg, sub, width // 2), jnp.bfloat16),
+            pltpu.SemaphoreType.DMA((2,)),
+            pltpu.SemaphoreType.DMA((2,)),
+            pltpu.SemaphoreType.DMA,
+            pltpu.SemaphoreType.DMA((n_msg,)),
+            pltpu.SemaphoreType.DMA((n_msg,)),
+            pltpu.SemaphoreType.DMA((n_msg,)),
+            pltpu.SemaphoreType.DMA((n_msg,)),
+            pltpu.SemaphoreType.DMA((2 * SUBS * nz,)),
+            pltpu.SemaphoreType.DMA((2 * SUBS * nz,)),
+        ],
+        compiler_params=pltpu.CompilerParams(collective_id=0, has_side_effects=True, vmem_limit_bytes=40 * 2**20),
+    )(attn, w_o, hidden, gain)
 
 
 def solution(mesh):
@@ -52,10 +273,7 @@
         k_new = write_slot(k_cache, k_rot, positions)
         v_new = write_slot(v_cache, v_local.reshape(n_rows, local_heads, head_dim), positions)
         attn = attend(q_rot, k_new, v_new, positions)
-        proj_part = jnp.dot(attn.reshape(n_rows, local_heads * head_dim), w_o, preferred_element_type=jnp.float32).astype(jnp.bfloat16)
-        a_out = lax.psum(proj_part, 'tp').astype(jnp.float32)
-        inv_out = lax.rsqrt(jnp.mean(a_out * a_out, axis=-1, keepdims=True) + NORM_EPS)
-        hidden_out = (hidden.astype(jnp.float32) + a_out * inv_out * post_norm_w).astype(jnp.bfloat16)
+        hidden_out = finish_call(mesh.shape['tp'], attn.reshape(n_rows, local_heads * head_dim), w_o, hidden, post_norm_w[None, :])
         return hidden_out, k_new, v_new
 
     cache_spec = P('dp', None, 'tp', None)

time: 231 us -> 158 us (0.68)
  waiting for transfers between devices: 114 us -> 0 us
  Pallas kernels: 0 us -> 63.5 us
  between operations: 14.3 us -> 0.91 us
  other arithmetic: 51.6 us -> 43 us
    psum x1 -> x0, waiting for transfers between devices: 114 us -> none  [local_step(): a_out = lax.psum(proj_part, 'tp').astype(jnp.float32)]
    pallas_call x0 -> x1, Pallas kernels: none -> 63.5 us  [finish_call(): pl.pallas_call(functools.partial(finish_kernel, n_tp), name='finish', out...]
    convert_element_type x1 -> x0, other arithmetic: 6.36 us -> none  [local_step(): (hidden.astype(jnp.float32) + a_out * inv_out * post_norm_w).astype(jnp.b...]
    dot_general x1 -> x0, matrix products: 3.28 us -> none  [local_step(): jnp.dot(attn.reshape(n_rows, local_heads * head_dim), w_o, preferred_elem...]
    reduce_sum x1 -> x0, other arithmetic: 3.23 us -> none  [local_step(): jnp.mean(a_out * a_out, axis=-1, keepdims=True) + NORM_EPS]
    dot_general x1, matrix products: 1.22 us -> 3.56 us  [attend(): jnp.einsum('bhs,bshd->bhd', probs, v_new, preferred_element_type=jnp.floa...]
  transfers between devices with their start and end apart: 1 -> 0, of which waited for: 1 -> 0; matrix products, arithmetic and copies ran while one was open for 0% -> 0% of each run, Pallas kernels for 0% -> 0%
where the time goes in v1:
time: 158 us
  Pallas kernels  63.5 us (40%)
  other arithmetic  43 us (27%)
  blocking collectives  29 us (18%)
  matrix products  13.5 us (9%)
  local copies, waits for them, and re-layouts  7.69 us (5%)
    pallas_call x1, Pallas kernels, finish_call(): pl.pallas_call(functools.partial(finish_kernel, n_tp), name='finish', out...  63.5 us
    psum x1, blocking collectives, local_step(): energy = lax.psum(energy, 'tp')  29 us
    unnamed x2, other arithmetic  25.7 us
    select_n x1, other arithmetic, write_slot(): return jnp.where(at_slot, new_vals[:, None], cache)  13.3 us
    dot_general x1, matrix products, local_step(): jnp.dot(hidden, w_v, preferred_element_type=jnp.float32)  4.16 us
    dot_general x1, matrix products, local_step(): jnp.dot(hidden, w_q, preferred_element_type=jnp.float32)  3.65 us
    dot_general x1, matrix products, attend(): jnp.einsum('bhs,bshd->bhd', probs, v_new, preferred_element_type=jnp.floa...  3.56 us

profile of v1, /device:TPU:21, one launch (start us, length us, event | category | flops | bytes accessed | tf_op | source)
XLA Modules:
  0.0 157.6 jit_solution(2601587313345133256)
XLA Ops:
  0.6 0.0 copy-start
  0.7 0.8 convert_element_type.56
  1.5 0.8 iota_compare_fusion.1
  2.3 0.1 copy.16
  2.4 0.5 multiply_cosine_fusion
  3.0 4.2 %convolution_convert_fusion = bf16[512,256]{0,1:T(8,128)(2,1)S(1)} fusion(bf16[512,4096]{1,0:T(8,128)(2,1)} %hid_ref.1, bf16[4096,256]{1,0:T(8,128)(2,1)} %param.14), kind=kOutput, calls=%fused_computation.7 | convolution fusion | flops 1073872896 | bytes 6553600 | tf_op jit(solution)/shard_map/dot_general | solution.py:265
  7.1 0.2 copy.18
  7.3 0.0 copy-done
  7.3 0.0 copy-start.1
  7.3 0.0 copy-start.8
  7.3 3.6 %multiply_reduce_fusion.2 = (f32[512]{0:T(512)S(1)}, f32[512,256]{0,1:T(8,128)S(1)}) fusion(bf16[512,4096]{1,0:T(8,128)(2,1)} %hid_ref.1, bf16[4096,256]{1,0:T(8,128)(2,1)S(1)} %copy-done), kind=kOutput, calls=%fused_computation.20 | convolution fusion | flops 1074265600 | bytes 6817792 | tf_op jit(solution)/shard_map/dot_general | solution.py:263
  11.0 0.0 copy-done.1
  11.0 0.4 copy-done.8
  11.5 0.0 copy-start.6
  11.5 0.0 copy-start.7
  11.5 2.1 %multiply_reduce_fusion.1 = (f32[512]{0:T(512)S(1)}, f32[512,256]{0,1:T(8,128)}) fusion(bf16[512,4096]{1,0:T(8,128)(2,1)S(1)} %copy-done.1, bf16[4096,256]{1,0:T(8,128)(2,1)S(1)} %copy-done.8), kind=kOutput, calls=%fused_computation.19 | convolution fusion | flops 1074265600 | bytes 6817792 | tf_op jit(solution)/shard_map/dot_general | solution.py:264
  13.6 29.0 %psum.7 = f32[2,512]{1,0:T(2,128)S(1)} all-reduce(f32[2,512]{1,0:T(2,128)S(1)} %pad_maximum_fusion.1), channel_id=1, replica_groups=mesh['dp'=4,'tp'=16] {'tp'}, use_global_device_ids=true, to_apply=%region_2.0 | all-reduce | flops 1024 | bytes 8192 | tf_op jit(solution)/shard_map/psum | solution.py:267
  42.6 0.0 copy-done.6
  42.6 1.1 multiply_convert_fusion
  43.7 0.0 copy-done.7
  43.7 0.1 multiply_convert_fusion.1
  43.9 0.1 convert.20
  43.9 0.1 convert.21
  44.0 0.2 subtract_convert_fusion
  44.2 0.8 maximum_convert_fusion
  44.9 0.2 copy.29
  45.2 1.1 copy.17
  46.3 0.0 copy-start.5
  46.3 13.3 %broadcast_select_fusion = bf16[512,16,2,128]{3,2,1,0:T(2,128)(2,1)} fusion(bf16[512,16,2,128]{3,2,1,0:T(2,128)(2,1)} %param.20, pred[512,16]{1,0:T(8,128)(4,1)S(1)} %get-tuple-element.16, bf16[512,2,128]{2,1,0:T(2,128)(2,1)S(1)} %copy.18), kind=kLoop, calls=%fused_computation.3 | loop fusion | flops 2097152 | bytes 8658944 | tf_op jit(solution)/shard_map/jit(_where)/select_n | solution.py:31
  59.6 0.0 copy-done.5
  59.6 25.0 %multiply_reduce_fusion = (f32[512,2,16]{1,2,0:T(8,128)}, bf16[512,16,2,128]{3,2,1,0:T(2,128)(2,1)}) fusion(f32[512,2,128]{2,1,0:T(2,128)S(1)} %copy.29, bf16[512,16,2,128]{3,2,1,0:T(2,128)(2,1)S(1)} %copy-done.5, bf16[512,2,128]{2,1,0:T(2,128)(2,1)S(1)} %copy.17, pred[512,16]{1,0:T(8,128)(4,1)S(1)} %get-tuple-element.16), kind=kLoop, calls=%fused_computation.2 | loop fusion | flops 8372224 | bytes 9248768
  84.6 2.8 %copy.25 = f32[512,2,16]{0,2,1:T(8,128)S(1)} copy(f32[512,2,16]{1,2,0:T(8,128)} %get-tuple-element.3) | data formatting | bytes 131072 | tf_op jit(solution)/shard_map/bhd,bshd->bhs/dot_general | solution.py:36
  87.4 0.0 copy-start.4
  87.5 0.4 copy.26
  87.9 0.0 copy-start.2
  87.9 0.0 copy-start.3
  87.9 3.6 %fusion.2 = f32[512,2,1,128]{3,2,1,0:T(1,128)S(1)} fusion(bf16[512,2,16,1]{2,3,1,0:T(2,128)(2,1)S(1)} %copy.26, bf16[512,16,2,128]{3,2,1,0:T(2,128)(2,1)} %broadcast_select_fusion), kind=kOutput, calls=%fused_computation.5 | convolution fusion | flops 4194304 | bytes 4751360 | tf_op jit(solution)/shard_map/bhs,bshd->bhd/dot_general | solution.py:40
  91.5 0.2 convert_element_type.62
  91.7 0.0 copy-done.4
  91.7 0.0 copy-done.2
  91.7 0.3 copy-done.3
  92.0 63.5 %finish.1 = bf16[512,4096]{1,0:T(8,128)(2,1)S(1)} custom-call(bf16[512,256]{1,0:T(8,128)(2,1)S(1)} %bitcast.27, bf16[256,4096]{1,0:T(8,128)(2,1)S(1)} %copy-done.3, bf16[512,4096]{1,0:T(8,128)(2,1)S(1)} %copy-done.2, f32[1,4096]{1,0:T(1,128)S(1)} %bitcast.28), custom_call_target="tpu_custom_call" | custom-call | tf_op jit(solution)/shard_map/finish/pallas_call | solution.py:232
  155.6 2.0 %copy.37 = bf16[512,4096]{1,0:T(8,128)(2,1)} copy(bf16[512,4096]{1,0:T(8,128)(2,1)S(1)} %finish.1) | data formatting | bytes 8388608
  (6 shorter events, 0.1 us)
Async XLA Ops:
  0.6 6.7 %copy-start = (bf16[4096,256]{1,0:T(8,128)(2,1)S(1)}, bf16[4096,256]{1,0:T(8,128)(2,1)}, u32[]{:S(2)}) copy-start(bf16[4096,256]{1,0:T(8,128)(2,1)} %param.12) | copy-start | bytes 6291460
  7.3 3.7 %copy-start.1 = (bf16[512,4096]{1,0:T(8,128)(2,1)S(1)}, bf16[512,4096]{1,0:T(8,128)(2,1)}, u32[]{:S(2)}) copy-start(bf16[512,4096]{1,0:T(8,128)(2,1)} %hid_ref.1) | copy-start | bytes 12582916
  7.3 4.1 %copy-start.8 = (bf16[4096,256]{1,0:T(8,128)(2,1)S(1)}, bf16[4096,256]{1,0:T(8,128)(2,1)}, u32[]{:S(2)}) copy-start(bf16[4096,256]{1,0:T(8,128)(2,1)} %param.13) | copy-start | bytes 6291460
  11.5 31.1 %copy-start.6 = (f32[256]{0:T(256)S(1)}, f32[256]{0:T(256)}, u32[]{:S(2)}) copy-start(f32[256]{0:T(256)} %param.17) | copy-start | bytes 3076
  11.5 32.3 %copy-start.7 = (f32[256]{0:T(256)S(1)}, f32[256]{0:T(256)}, u32[]{:S(2)}) copy-start(f32[256]{0:T(256)} %param.16) | copy-start | bytes 3076
  46.3 13.3 %copy-start.5 = (bf16[512,16,2,128]{3,2,1,0:T(2,128)(2,1)S(1)}, bf16[512,16,2,128]{3,2,1,0:T(2,128)(2,1)}, u32[]{:S(2)}) copy-start(bf16[512,16,2,128]{3,2,1,0:T(2,128)(2,1)} %param.19) | copy-start | bytes 12582916
  87.4 4.3 %copy-start.4 = (f32[4096]{0:T(1024)S(1)}, f32[4096]{0:T(1024)}, u32[]{:S(2)}) copy-start(f32[4096]{0:T(1024)} %param.18) | copy-start | bytes 49156
  87.9 3.8 %copy-start.2 = (bf16[512,4096]{1,0:T(8,128)(2,1)S(1)}, bf16[512,4096]{1,0:T(8,128)(2,1)}, u32[]{:S(2)}) copy-start(bf16[512,4096]{1,0:T(8,128)(2,1)} %hid_ref.1) | copy-start | bytes 12582916
  87.9 4.1 %copy-start.3 = (bf16[256,4096]{1,0:T(8,128)(2,1)S(1)}, bf16[256,4096]{1,0:T(8,128)(2,1)}, u32[]{:S(2)}) copy-start(bf16[256,4096]{1,0:T(8,128)(2,1)} %w_ref.1) | copy-start | bytes 6291460

commit v2 on v1

--- a/solution.py
+++ b/solution.py
@@ -25,19 +25,80 @@
     return jnp.concatenate([first * cos_tab - second * sin_tab, second * cos_tab + first * sin_tab], axis=-1).astype(jnp.bfloat16)
 
 
-def write_slot(cache, new_vals, positions):
-    slot_ids = jnp.arange(cache.shape[1], dtype=jnp.int32)
-    at_slot = (slot_ids[None, :] == positions[:, None])[:, :, None, None]
-    return jnp.where(at_slot, new_vals[:, None], cache)
-
-
-def attend(q_rot, k_new, v_new, positions):
-    slot_ids = jnp.arange(k_new.shape[1], dtype=jnp.int32)
-    scores = jnp.einsum('bhd,bshd->bhs', q_rot, k_new, preferred_element_type=jnp.float32) * k_new.shape[3] ** -0.5
-    valid = (slot_ids[None, :] <= positions[:, None])[:, None, :]
-    scores = jnp.where(valid, scores, -1e30)
-    probs = jax.nn.softmax(scores, axis=-1).astype(jnp.bfloat16)
-    return jnp.einsum('bhs,bshd->bhd', probs, v_new, preferred_element_type=jnp.float32).astype(jnp.bfloat16)
+ROW_BLOCK = 64
+GROUP = 8
+
+
+def attend_kernel(slots, heads, pos_ref, q_ref, k_ref, v_ref, posb_ref, kc_ref, vc_ref, o_ref, kn_ref, vn_ref, kf, vf):
+    block = q_ref.shape[0]
+    dim = q_ref.shape[1] // heads
+    lines = slots * heads
+    step = pl.program_id(0)
+    kf[...] = k_ref[...].astype(jnp.float32)
+    vf[...] = v_ref[...].astype(jnp.float32)
+    line = lax.broadcasted_iota(jnp.int32, (lines // 2, dim), 0)
+    first = lax.rem(line, heads) == 0
+    slot_of = [(line // heads + part * (slots // 2)).astype(jnp.float32).astype(jnp.bfloat16) for part in range(2)]
+
+    def insert(r):
+        p = jnp.full((lines // 2, dim), pos_ref[step * block + r].astype(jnp.float32)).astype(jnp.bfloat16)
+        for src, old, new in ((kf, kc_ref, kn_ref), (vf, vc_ref, vn_ref)):
+            h0 = jnp.broadcast_to(src[pl.ds(r, 1), 0:dim], (lines // 2, dim))
+            h1 = jnp.broadcast_to(src[pl.ds(r, 1), dim:2 * dim], (lines // 2, dim))
+            fresh = jnp.where(first, h0, h1).astype(jnp.bfloat16)
+            for part in range(2):
+                at = pl.ds(r * lines + part * (lines // 2), lines // 2)
+                new[at, :] = jnp.where(slot_of[part] == p, fresh, old[at, :])
+
+    for r in range(block):
+        insert(r)
+
+    n_groups = block // GROUP
+    wide = GROUP * lines
+    m = lax.broadcasted_iota(jnp.int32, (heads * GROUP, wide), 0)
+    n = lax.broadcasted_iota(jnp.int32, (heads * GROUP, wide), 1)
+    own = (lax.rem(m, GROUP) == n // lines) & (m // GROUP == lax.rem(n, heads))
+    slot = jnp.where(own, (lax.rem(n, lines) // heads).astype(jnp.float32), 1e9)
+    scores = []
+    for g in range(n_groups):
+        rows = slice(g * GROUP, (g + 1) * GROUP)
+        q = jnp.concatenate([q_ref[rows, h * dim:(h + 1) * dim] for h in range(heads)], axis=0)
+        keys = kn_ref[g * wide:(g + 1) * wide, :]
+        s = lax.dot_general(q, keys, (((1,), (1,)), ((), ())), preferred_element_type=jnp.float32) * dim ** -0.5
+        at = jnp.concatenate([posb_ref[rows, :]] * heads, axis=0)
+        at = jnp.concatenate([at] * (wide // at.shape[1]), axis=1)
+        scores.append(jnp.where(slot <= at, s, -1e30))
+    for g in range(n_groups):
+        s = scores[g]
+        e = jnp.exp(s - jnp.max(s, axis=-1, keepdims=True))
+        probs = (e / jnp.sum(e, axis=-1, keepdims=True)).astype(jnp.bfloat16)
+        o = jnp.dot(probs, vn_ref[g * wide:(g + 1) * wide, :], preferred_element_type=jnp.float32).astype(jnp.bfloat16)
+        for h in range(heads):
+            o_ref[g * GROUP:(g + 1) * GROUP, h * dim:(h + 1) * dim] = o[h * GROUP:(h + 1) * GROUP]
+
+
+def attend_call(q, k, v, posb, positions, k_cache, v_cache):
+    n_rows, slots, heads, dim = k_cache.shape
+    lines = slots * heads
+    flat = (n_rows * lines, dim)
+    block = ROW_BLOCK
+    row_spec = pl.BlockSpec((block, heads * dim), lambda i, pos: (i, 0))
+    cache_spec = pl.BlockSpec((block * lines, dim), lambda i, pos: (i, 0))
+    o, k_new, v_new = pl.pallas_call(
+        functools.partial(attend_kernel, slots, heads),
+        name="attend",
+        out_shape=[jax.ShapeDtypeStruct((n_rows, heads * dim), jnp.bfloat16),
+                   jax.ShapeDtypeStruct(flat, jnp.bfloat16), jax.ShapeDtypeStruct(flat, jnp.bfloat16)],
+        grid_spec=pltpu.PrefetchScalarGridSpec(
+            num_scalar_prefetch=1,
+            grid=(n_rows // block,),
+            in_specs=[row_spec, row_spec, row_spec, pl.BlockSpec((block, dim), lambda i, pos: (i, 0)), cache_spec, cache_spec],
+            out_specs=[row_spec, cache_spec, cache_spec],
+            scratch_shapes=[pltpu.VMEM((block, heads * dim), jnp.float32), pltpu.VMEM((block, heads * dim), jnp.float32)],
+        ),
+        compiler_params=pltpu.CompilerParams(vmem_limit_bytes=24 * 2**20),
+    )(positions, q, k, v, posb, k_cache.reshape(flat), v_cache.reshape(flat))
+    return o, k_new.reshape(k_cache.shape), v_new.reshape(v_cache.shape)
 
 
 MESH = pl.DeviceIdType.MESH
@@ -270,10 +331,9 @@
         k_normed = (k_local * inv_rms[1][:, None] * k_norm_w).astype(jnp.bfloat16).reshape(n_rows, local_heads, head_dim)
         q_rot = apply_rope(q_normed, positions)
         k_rot = apply_rope(k_normed, positions)
-        k_new = write_slot(k_cache, k_rot, positions)
-        v_new = write_slot(v_cache, v_local.reshape(n_rows, local_heads, head_dim), positions)
-        attn = attend(q_rot, k_new, v_new, positions)
-        hidden_out = finish_call(mesh.shape['tp'], attn.reshape(n_rows, local_heads * head_dim), w_o, hidden, post_norm_w[None, :])
+        posb = jnp.broadcast_to(positions.astype(jnp.float32)[:, None], (n_rows, head_dim))
+        attn, k_new, v_new = attend_call(q_rot.reshape(n_rows, -1), k_rot.reshape(n_rows, -1), v_local, posb, positions, k_cache, v_cache)
+        hidden_out = finish_call(mesh.shape['tp'], attn, w_o, hidden, post_norm_w[None, :])
         return hidden_out, k_new, v_new
 
     cache_spec = P('dp', None, 'tp', None)

time: 158 us -> 129 us (0.82)
  other arithmetic: 43 us -> 7.85 us
  Pallas kernels: 63.5 us -> 69.8 us
  matrix products: 13.5 us -> 7.67 us
  local copies, waits for them, and re-layouts: 7.69 us -> 13.4 us
    unnamed x2 -> x0, other arithmetic: 25.7 us -> none
    select_n x1 -> x0, other arithmetic: 13.3 us -> none  [write_slot(): return jnp.where(at_slot, new_vals[:, None], cache)]
    unnamed x21 -> x29, local copies, waits for them, and re-layouts: 3.06 us -> 11.6 us
    pallas_call x0 -> x1, Pallas kernels: none -> 6.4 us  [attend_call(): pl.pallas_call(functools.partial(attend_kernel, slots, heads), name='atte...]
    dot_general x1 -> x0, matrix products: 3.56 us -> none  [attend(): jnp.einsum('bhs,bshd->bhd', probs, v_new, preferred_element_type=jnp.floa...]
    dot_general x1 -> x0, local copies, waits for them, and re-layouts: 2.85 us -> none  [attend(): jnp.einsum('bhd,bshd->bhs', q_rot, k_new, preferred_element_type=jnp.floa...]
    another operation x1, other arithmetic: 0.17 us -> 2.5 us
    dot_general x1, matrix products: 3.65 us -> 1.33 us  [local_step(): jnp.dot(hidden, w_q, preferred_element_type=jnp.float32)]
where the time goes in v2:
time: 129 us
  Pallas kernels  69.8 us (54%)
  blocking collectives  29 us (22%)
  local copies, waits for them, and re-layouts  13.4 us (10%)
  other arithmetic  7.85 us (6%)
  matrix products  7.67 us (6%)
    pallas_call x1, Pallas kernels, finish_call(): pl.pallas_call(functools.partial(finish_kernel, n_tp), name='finish', out...  63.4 us
    psum x1, blocking collectives, local_step(): energy = lax.psum(energy, 'tp')  29 us
    unnamed x29, local copies, waits for them, and re-layouts  11.6 us
    pallas_call x1, Pallas kernels, attend_call(): pl.pallas_call(functools.partial(attend_kernel, slots, heads), name='atte...  6.4 us
    dot_general x1, matrix products, local_step(): jnp.dot(hidden, w_v, preferred_element_type=jnp.float32)  4.25 us

profile of v2, /device:TPU:21, one launch (start us, length us, event | category | flops | bytes accessed | tf_op | source)
XLA Modules:
  0.0 128.5 jit_solution(8761940824926631062)
XLA Ops:
  0.6 0.0 copy-start
  0.7 0.8 convert_element_type.55
  1.5 0.1 broadcast_in_dim.4.posb_ref
  1.6 0.0 copy-start.3
  1.6 4.2 %convolution_convert_fusion.v_ref = bf16[512,256]{1,0:T(8,128)(2,1)S(1)} fusion(bf16[512,4096]{1,0:T(8,128)(2,1)} %hid_ref.1, bf16[4096,256]{1,0:T(8,128)(2,1)} %param.14), kind=kOutput, calls=%fused_computation | convolution fusion | flops 1073872896 | bytes 6553600 | tf_op jit(solution)/shard_map/dot_general | solution.py:326
  5.9 1.8 %multiply_cosine_fusion = (f32[512,64]{1,0:T(8,128)}, f32[512,64]{1,0:T(8,128)}) fusion(f32[64]{0:T(128)S(1)} %multiply_power_fusion, f32[512]{0:T(512)S(1)} %convert_element_type.55), kind=kLoop, calls=%fused_computation.14 | loop fusion | flops 32768 | bytes 264448 | tf_op jit(solution)/shard_map/cos | solution.py:20
  7.7 0.0 copy-done
  7.7 0.0 copy-done.3
  7.7 0.0 copy-start.10
  7.7 1.3 %multiply_reduce_fusion.1 = (f32[512]{0:T(512)S(1)}, f32[512,256]{0,1:T(8,128)S(1)}) fusion(bf16[512,4096]{1,0:T(8,128)(2,1)S(1)} %copy-done.3, bf16[4096,256]{1,0:T(8,128)(2,1)S(1)} %copy-done), kind=kOutput, calls=%fused_computation.12 | convolution fusion | flops 1074265600 | bytes 6817792 | tf_op jit(solution)/shard_map/dot_general | solution.py:324
  9.0 0.3 copy-done.10
  9.3 0.0 copy-start.8
  9.3 0.0 copy-start.9
  9.3 2.1 %multiply_reduce_fusion = (f32[512]{0:T(512)S(1)}, f32[512,256]{0,1:T(8,128)}) fusion(bf16[512,4096]{1,0:T(8,128)(2,1)S(1)} %copy-done.3, bf16[4096,256]{1,0:T(8,128)(2,1)S(1)} %copy-done.10), kind=kOutput, calls=%fused_computation.11 | convolution fusion | flops 1074265600 | bytes 6817792 | tf_op jit(solution)/shard_map/dot_general | solution.py:325
  11.4 29.0 %psum.7 = f32[2,512]{1,0:T(2,128)S(1)} all-reduce(f32[2,512]{1,0:T(2,128)S(1)} %pad_maximum_fusion.2), channel_id=1, replica_groups=mesh['dp'=4,'tp'=16] {'tp'}, use_global_device_ids=true, to_apply=%region_2.0 | all-reduce | flops 1024 | bytes 8192 | tf_op jit(solution)/shard_map/psum | solution.py:328
  40.4 0.0 copy-done.8
  40.4 1.1 multiply_convert_fusion
  41.6 0.0 copy-done.9
  41.6 0.1 multiply_convert_fusion.1
  41.7 0.8 fusion.3
  42.5 1.2 copy.19
  43.7 0.8 fusion.2
  44.6 0.0 copy-start.7
  44.6 2.0 %copy.21 = f32[512,2,64]{2,1,0:T(2,128)} copy(f32[512,2,64]{0,2,1:T(8,128)} %get-tuple-element.15) | data formatting | bytes 524288
  46.5 1.9 %copy.20 = f32[512,2,64]{2,1,0:T(2,128)} copy(f32[512,2,64]{0,2,1:T(8,128)} %get-tuple-element.16) | data formatting | bytes 524288
  48.5 1.9 %copy.18 = f32[512,2,64]{2,1,0:T(2,128)} copy(f32[512,2,64]{0,2,1:T(8,128)} %get-tuple-element.18) | data formatting | bytes 524288
  50.4 0.0 copy-start.1
  50.4 2.5 %subtract_convert_fusion = (bf16[512,2,64]{2,1,0:T(2,128)(2,1)S(1)}, bf16[512,2,64]{2,1,0:T(2,128)(2,1)S(1)}, bf16[512,2,64]{2,1,0:T(2,128)(2,1)S(1)}, bf16[512,2,64]{2,1,0:T(2,128)(2,1)S(1)}) fusion(f32[512,2,64]{2,1,0:T(2,128)} %copy.21, f32[512,2,64]{2,1,0:T(2,128)} %copy.20, f32[512,64]{1,0:T(8,128)} %get-tuple-element.22, ...), kind=kLoop, calls=%fused_computation.6 | loop fusion | flops 1048576 | bytes 1835008 | tf_op jit(solution)/shard_map/convert.2
  53.0 1.4 %pad_maximum_fusion = (bf16[512,2,128]{2,1,0:T(2,128)(2,1)S(1)}, bf16[512,2,128]{2,1,0:T(2,128)(2,1)S(1)}) fusion(bf16[512,2,64]{2,1,0:T(2,128)(2,1)S(1)} %get-tuple-element.13, bf16[512,2,64]{2,1,0:T(2,128)(2,1)S(1)} %get-tuple-element.14, bf16[512,2,64]{2,1,0:T(2,128)(2,1)S(1)} %get-tuple-element.10, bf16[512,2,64]{2,1,0:T(2,128)(2,1)S(1)} %get-tuple-element.9), kind=kLoop, calls=%fused_computation.17 | loop fusion | flops 1048576 | bytes 1048576 | tf_op jit(solution)/shard_map/concatenate | solution.py:25
  54.5 0.0 copy-done.7
  54.5 0.0 copy-done.1
  54.5 0.0 copy-start.2
  54.5 2.2 %copy-done.2 = bf16[512,16,2,128]{3,2,1,0:T(2,128)(2,1)S(1)} copy-done((bf16[512,16,2,128]{3,2,1,0:T(2,128)(2,1)S(1)}, bf16[512,16,2,128]{3,2,1,0:T(2,128)(2,1)}, u32[]{:S(2)}) %copy-start.2) | copy-done | bytes 4194328
  56.7 0.0 copy-start.4
  56.7 0.0 copy-start.5
  56.7 0.0 copy-start.6
  56.7 6.4 %attend.1 = (bf16[512,256]{1,0:T(8,128)(2,1)S(1)}, bf16[16384,128]{1,0:T(8,128)(2,1)}, bf16[16384,128]{1,0:T(8,128)(2,1)}) custom-call(s32[512]{0:T(512)S(1)} %copy-done.7, bf16[512,256]{1,0:T(8,128)(2,1)S(1)} %bitcast.29, bf16[512,256]{1,0:T(8,128)(2,1)S(1)} %bitcast.30, bf16[512,256]{1,0:T(8,128)(2,1)S(1)} %convolution_convert_fusion.v_ref, ...), custom_call_target="tpu_custom_call" | custom-call | tf_op jit(solution)/shard_map/attend/pallas_call | solution.py:87
  63.1 0.0 copy-done.4
  63.1 0.0 copy-done.5
  63.1 0.0 copy-done.6
  63.1 63.4 %finish.1 = bf16[512,4096]{1,0:T(8,128)(2,1)S(1)} custom-call(bf16[512,256]{1,0:T(8,128)(2,1)S(1)} %get-tuple-element.6.o_ref, bf16[256,4096]{1,0:T(8,128)(2,1)S(1)} %copy-done.5, bf16[512,4096]{1,0:T(8,128)(2,1)S(1)} %copy-done.4, f32[1,4096]{1,0:T(1,128)S(1)} %bitcast.31), custom_call_target="tpu_custom_call" | custom-call | tf_op jit(solution)/shard_map/finish/pallas_call | solution.py:293
  126.5 2.0 %copy.29 = bf16[512,4096]{1,0:T(8,128)(2,1)} copy(bf16[512,4096]{1,0:T(8,128)(2,1)S(1)} %finish.1) | data formatting | bytes 8388608
  (6 shorter events, 0.1 us)
Async XLA Ops:
  0.6 7.1 %copy-start = (bf16[4096,256]{1,0:T(8,128)(2,1)S(1)}, bf16[4096,256]{1,0:T(8,128)(2,1)}, u32[]{:S(2)}) copy-start(bf16[4096,256]{1,0:T(8,128)(2,1)} %param.12) | copy-start | bytes 6291460
  1.6 6.1 %copy-start.3 = (bf16[512,4096]{1,0:T(8,128)(2,1)S(1)}, bf16[512,4096]{1,0:T(8,128)(2,1)}, u32[]{:S(2)}) copy-start(bf16[512,4096]{1,0:T(8,128)(2,1)} %hid_ref.1) | copy-start | bytes 12582916
  7.7 1.6 %copy-start.10 = (bf16[4096,256]{1,0:T(8,128)(2,1)S(1)}, bf16[4096,256]{1,0:T(8,128)(2,1)}, u32[]{:S(2)}) copy-start(bf16[4096,256]{1,0:T(8,128)(2,1)} %param.13) | copy-start | bytes 6291460
  9.3 31.1 %copy-start.8 = (f32[256]{0:T(256)S(1)}, f32[256]{0:T(256)}, u32[]{:S(2)}) copy-start(f32[256]{0:T(256)} %param.17) | copy-start | bytes 3076
  9.3 32.3 %copy-start.9 = (f32[256]{0:T(256)S(1)}, f32[256]{0:T(256)}, u32[]{:S(2)}) copy-start(f32[256]{0:T(256)} %param.16) | copy-start | bytes 3076
  44.6 9.9 %copy-start.7 = (s32[512]{0:T(512)S(1)}, s32[512]{0:T(512)}, u32[]{:S(2)}) copy-start(s32[512]{0:T(512)} %pos_ref.1) | copy-start | bytes 6148
  50.4 4.0 %copy-start.1 = (bf16[512,16,2,128]{3,2,1,0:T(2,128)(2,1)S(1)}, bf16[512,16,2,128]{3,2,1,0:T(2,128)(2,1)}, u32[]{:S(2)}) copy-start(bf16[512,16,2,128]{3,2,1,0:T(2,128)(2,1)} %param.19) | copy-start | bytes 12582916
  54.5 2.2 %copy-start.2 = (bf16[512,16,2,128]{3,2,1,0:T(2,128)(2,1)S(1)}, bf16[512,16,2,128]{3,2,1,0:T(2,128)(2,1)}, u32[]{:S(2)}) copy-start(bf16[512,16,2,128]{3,2,1,0:T(2,128)(2,1)} %param.20) | copy-start | bytes 12582916
  56.7 6.4 %copy-start.4 = (bf16[512,4096]{1,0:T(8,128)(2,1)S(1)}, bf16[512,4096]{1,0:T(8,128)(2,1)}, u32[]{:S(2)}) copy-start(bf16[512,4096]{1,0:T(8,128)(2,1)} %hid_ref.1) | copy-start | bytes 12582916
  56.7 6.4 %copy-start.5 = (bf16[256,4096]{1,0:T(8,128)(2,1)S(1)}, bf16[256,4096]{1,0:T(8,128)(2,1)}, u32[]{:S(2)}) copy-start(bf16[256,4096]{1,0:T(8,128)(2,1)} %w_ref.1) | copy-start | bytes 6291460
  56.7 6.4 %copy-start.6 = (f32[4096]{0:T(1024)S(1)}, f32[4096]{0:T(1024)}, u32[]{:S(2)}) copy-start(f32[4096]{0:T(1024)} %param.18) | copy-start | bytes 49156

commit v3 on v2

--- a/solution.py
+++ b/solution.py
@@ -2,6 +2,7 @@
 
 import jax
 import jax.numpy as jnp
+import numpy as np
 from jax import lax
 from jax.experimental import pallas as pl
 from jax.experimental.pallas import tpu as pltpu
@@ -12,17 +13,156 @@
 OUT_VMEM = True
 
 
-def apply_rope(heads_val, positions):
-    head_dim = heads_val.shape[-1]
-    half = head_dim // 2
-    inv_freq = ROPE_BASE ** (-2.0 * jnp.arange(half, dtype=jnp.float32) / head_dim)
-    angles = positions.astype(jnp.float32)[:, None, None] * inv_freq[None, None, :]
-    cos_tab = jnp.cos(angles)
-    sin_tab = jnp.sin(angles)
-    wide = heads_val.astype(jnp.float32)
-    first = wide[..., :half]
-    second = wide[..., half:]
-    return jnp.concatenate([first * cos_tab - second * sin_tab, second * cos_tab + first * sin_tab], axis=-1).astype(jnp.bfloat16)
+MESH = pl.DeviceIdType.MESH
+DEPTH_CUTS = 4
+TABLE_ROWS = 128
+
+
+def rope_table(slots, dim):
+    half = dim // 2
+    inv_freq = np.float32(ROPE_BASE) ** (np.float32(-2.0) * np.arange(half, dtype=np.float32) / np.float32(dim))
+    angles = (np.arange(slots, dtype=np.float32)[:, None] * inv_freq.astype(np.float32)[None, :]).astype(np.float64)
+    cos_tab, sin_tab = np.cos(angles), np.sin(angles)
+    rest = np.concatenate([cos_tab, cos_tab, -sin_tab, sin_tab], axis=1).astype(np.float32)
+    out = np.zeros((TABLE_ROWS, 2 * dim), np.float32)
+    for part in range(3):
+        high = rest.astype(jnp.bfloat16).astype(np.float32)
+        out[part * slots:(part + 1) * slots] = high
+        rest = rest - high
+    return jnp.asarray(out, dtype=jnp.bfloat16)
+
+
+def project_kernel(n_tp, slots, dim, pos_ref, table_ref, qg_ref, kg_ref, hid_ref, wq_ref, wk_ref, wv_ref, wo_ref,
+                   q_ref, k_ref, v_ref, posb_ref, wo_in,
+                   hid, wqk, wv, acc, vacc, cosb, sinb, e_mine, e_in,
+                   in_sem, v_sem, e_send, e_recv, w_sem):
+    t = lax.axis_index("tp")
+    mate = t + 1 - 2 * lax.rem(t, 2)
+    n_rows, width = hid_ref.shape
+    local = wq_ref.shape[1]
+    heads = local // dim
+    cut = width // DEPTH_CUTS
+    barrier = pltpu.get_barrier_semaphore()
+    for off in range(1, n_tp):
+        pl.semaphore_signal(barrier, inc=1, device_id={"tp": lax.rem(t + off, n_tp)}, device_id_type=MESH)
+
+    loads = []
+    for c in range(DEPTH_CUTS):
+        at = pl.ds(c * cut, cut)
+        loads.append([
+            pltpu.make_async_copy(hid_ref.at[:, at], hid.at[c], in_sem.at[c, 0]),
+            pltpu.make_async_copy(wq_ref.at[at, :], wqk.at[c, :, pl.ds(0, local)], in_sem.at[c, 1]),
+            pltpu.make_async_copy(wk_ref.at[at, :], wqk.at[c, :, pl.ds(local, local)], in_sem.at[c, 2])])
+    v_loads = [pltpu.make_async_copy(wv_ref.at[pl.ds(c * cut, cut), :], wv.at[c], v_sem.at[c]) for c in range(DEPTH_CUTS)]
+    for group in loads:
+        for copy in group:
+            copy.start()
+    for copy in v_loads:
+        copy.start()
+
+    w_copy = pltpu.make_async_remote_copy(wo_ref, wo_in, w_sem.at[0], w_sem.at[1], device_id={"tp": mate}, device_id_type=MESH)
+    for c in range(DEPTH_CUTS):
+        for copy in loads[c]:
+            copy.wait()
+        part = jnp.dot(hid[c], wqk[c], preferred_element_type=jnp.float32)
+        if c == 0:
+            acc[...] = part
+        else:
+            acc[...] += part
+        if c == DEPTH_CUTS - 2:
+            pl.semaphore_wait(barrier, n_tp - 1)
+            w_copy.start()
+
+    lanes = e_mine.shape[1]
+    blocks = n_rows // lanes
+    ones = jnp.ones((8, local), jnp.bfloat16)
+    nt = (((1,), (1,)), ((), ()))
+    for i in range(2):
+        rounded = acc[:, i * local:(i + 1) * local].astype(jnp.bfloat16).astype(jnp.float32)
+        square = rounded * rounded
+        high = square.astype(jnp.bfloat16)
+        low = (square - high.astype(jnp.float32)).astype(jnp.bfloat16)
+        energy = (lax.dot_general(ones, high, nt, preferred_element_type=jnp.float32)
+                  + lax.dot_general(ones, low, nt, preferred_element_type=jnp.float32))
+        for b in range(blocks):
+            e_mine[i * blocks + b:i * blocks + b + 1, :] = energy[0:1, b * lanes:(b + 1) * lanes]
+    sends = [pltpu.make_async_remote_copy(
+        e_mine, e_in.at[off], e_send.at[off], e_recv.at[off],
+        device_id={"tp": lax.rem(t + off, n_tp)}, device_id_type=MESH) for off in range(1, n_tp)]
+    for copy in sends:
+        copy.start()
+
+    for c in range(DEPTH_CUTS):
+        v_loads[c].wait()
+        part = jnp.dot(hid[c], wv[c], preferred_element_type=jnp.float32)
+        if c == 0:
+            vacc[...] = part
+        elif c < DEPTH_CUTS - 1:
+            vacc[...] += part
+        else:
+            v_ref[...] = (vacc[...] + part).astype(jnp.bfloat16)
+    lane = lax.broadcasted_iota(jnp.int32, (lanes, TABLE_ROWS), 1)
+    which = jnp.where(lane < 3 * slots, lax.rem(lane, slots), -1).astype(jnp.float32)
+    for b in range(blocks):
+        at = slice(b * lanes, (b + 1) * lanes)
+        column = jnp.broadcast_to(pos_ref[b:b + 1, :].astype(jnp.float32), (lanes, lanes)).T
+        posb_ref[at, :] = column
+        hot = jnp.where(which == column, 1.0, 0.0).astype(jnp.bfloat16)
+        factors = jnp.dot(hot, table_ref[...], preferred_element_type=jnp.float32)
+        cosb[at, :] = factors[:, :dim]
+        sinb[at, :] = factors[:, dim:]
+
+    total = e_mine[...]
+    for i, copy in enumerate(sends):
+        copy.wait_recv()
+        total = total + e_in[i + 1]
+    inv = lax.rsqrt(total / width + NORM_EPS)
+    for b in range(blocks):
+        at = slice(b * lanes, (b + 1) * lanes)
+        for i, (gain, out) in enumerate(((qg_ref, q_ref), (kg_ref, k_ref))):
+            scale = jnp.broadcast_to(inv[i * blocks + b:i * blocks + b + 1, :], (lanes, lanes)).T
+            for h in range(heads):
+                cols = slice(h * dim, (h + 1) * dim)
+                x = acc[at, i * local + h * dim:i * local + (h + 1) * dim].astype(jnp.bfloat16).astype(jnp.float32)
+                x = (x * scale * gain[:, cols]).astype(jnp.bfloat16).astype(jnp.float32)
+                out[at, cols] = (x * cosb[at, :] + pltpu.roll(x, dim // 2, 1) * sinb[at, :]).astype(jnp.bfloat16)
+    for copy in sends:
+        copy.wait_send()
+    w_copy.wait()
+
+
+def project_call(n_tp, hidden, w_q, w_k, w_v, w_o, q_gain, k_gain, positions, slots, dim):
+    n_rows, width = hidden.shape
+    local = w_q.shape[1]
+    lanes = 128
+    cut = width // DEPTH_CUTS
+    vmem, hbm = pl.BlockSpec(memory_space=pltpu.VMEM), pl.BlockSpec(memory_space=pltpu.HBM)
+    return pl.pallas_call(
+        functools.partial(project_kernel, n_tp, slots, dim),
+        name="project",
+        out_shape=[pltpu.VMEM((n_rows, local), jnp.bfloat16)] * 3
+        + [pltpu.VMEM((n_rows, lanes), jnp.float32), pltpu.VMEM(w_o.shape, jnp.bfloat16)],
+        in_specs=[vmem] * 4 + [hbm] * 5,
+        out_specs=[vmem] * 5,
+        scratch_shapes=[
+            pltpu.VMEM((DEPTH_CUTS, n_rows, cut), jnp.bfloat16),
+            pltpu.VMEM((DEPTH_CUTS, cut, 2 * local), jnp.bfloat16),
+            pltpu.VMEM((DEPTH_CUTS, cut, local), jnp.bfloat16),
+            pltpu.VMEM((n_rows, 2 * local), jnp.float32),
+            pltpu.VMEM((n_rows, local), jnp.float32),
+            pltpu.VMEM((n_rows, dim), jnp.float32),
+            pltpu.VMEM((n_rows, dim), jnp.float32),
+            pltpu.VMEM((2 * n_rows // lanes, lanes), jnp.float32),
+            pltpu.VMEM((n_tp, 2 * n_rows // lanes, lanes), jnp.float32),
+            pltpu.SemaphoreType.DMA((DEPTH_CUTS, 3)),
+            pltpu.SemaphoreType.DMA((DEPTH_CUTS,)),
+            pltpu.SemaphoreType.DMA((n_tp,)),
+            pltpu.SemaphoreType.DMA((n_tp,)),
+            pltpu.SemaphoreType.DMA((2,)),
+        ],
+        compiler_params=pltpu.CompilerParams(collective_id=1, has_side_effects=True, vmem_limit_bytes=24 * 2**20),
+        cost_estimate=pl.CostEstimate(flops=6 * n_rows * width * local, bytes_accessed=2 * (n_rows * width + 3 * width * local), transcendentals=0),
+    )(positions.reshape(n_rows // lanes, lanes), rope_table(slots, dim), q_gain, k_gain, hidden, w_q, w_k, w_v, w_o)
 
 
 ROW_BLOCK = 64
@@ -101,13 +241,12 @@
     return o, k_new.reshape(k_cache.shape), v_new.reshape(v_cache.shape)
 
 
-MESH = pl.DeviceIdType.MESH
 SUBS = 2
 LAG = 2
 
 
-def finish_kernel(n_tp, o_ref, w_ref, hid_ref, gain_ref, out_ref,
-                  o_in, w_in, hid, share, rs_in, rs_out,
+def finish_kernel(n_tp, o_ref, w_ref, w_in, hid_ref, gain_ref, out_ref,
+                  o_in, hid, share, rs_in, rs_out,
                   x_send, x_recv, h_sem, rs_send, rs_recv, ag_send, ag_recv, d2d_send, d2d_recv):
     nz = n_tp // 2
     t = lax.axis_index("tp")
@@ -134,12 +273,9 @@
 
     o_copy = pltpu.make_async_remote_copy(
         o_ref.at[pl.ds(pl.multiple_of((1 - k) * half_rows, half_rows), half_rows), :], o_in,
-        x_send.at[0], x_recv.at[0], device_id={"tp": mate}, device_id_type=MESH)
-    w_copy = pltpu.make_async_remote_copy(w_ref, w_in, x_send.at[1], x_recv.at[1], device_id={"tp": mate}, device_id_type=MESH)
+        x_send, x_recv, device_id={"tp": mate}, device_id_type=MESH)
     o_copy.start()
-    w_copy.start()
     o_copy.wait_recv()
-    w_copy.wait_recv()
 
     tile = min(1024, width)
 
@@ -270,7 +406,6 @@
                 stage(g, s)
 
     o_copy.wait_send()
-    w_copy.wait_send()
     for (d, c, h, s) in slots:
         rs_message(d, c, h, s).wait_send()
         ag_message(d, c, h, s).wait_send()
@@ -282,7 +417,7 @@
         copy.wait_recv()
 
 
-def finish_call(n_tp, attn, w_o, hidden, gain):
+def finish_call(n_tp, attn, w_o, w_mate, hidden, gain):
     n_rows, width = hidden.shape
     depth = w_o.shape[0]
     nz = n_tp // 2
@@ -294,17 +429,16 @@
         functools.partial(finish_kernel, n_tp),
         name="finish",
         out_shape=pltpu.VMEM((n_rows, width), jnp.bfloat16) if OUT_VMEM else jax.ShapeDtypeStruct((n_rows, width), jnp.bfloat16),
-        in_specs=[vmem, vmem, pl.BlockSpec(memory_space=pl.ANY), vmem],
+        in_specs=[vmem, vmem, vmem, pl.BlockSpec(memory_space=pltpu.HBM), vmem],
         out_specs=vmem,
         scratch_shapes=[
             pltpu.VMEM((half_rows, depth), jnp.bfloat16),
-            pltpu.VMEM((depth, width), jnp.bfloat16),
             pltpu.VMEM((rows, width), jnp.bfloat16),
             pltpu.VMEM((nz, rows, width), jnp.float32),
             pltpu.VMEM((n_msg, sub, width // 2), jnp.bfloat16),
             pltpu.VMEM((n_msg, sub, width // 2), jnp.bfloat16),
-            pltpu.SemaphoreType.DMA((2,)),
-            pltpu.SemaphoreType.DMA((2,)),
+            pltpu.SemaphoreType.DMA,
+            pltpu.SemaphoreType.DMA,
             pltpu.SemaphoreType.DMA,
             pltpu.SemaphoreType.DMA((n_msg,)),
             pltpu.SemaphoreType.DMA((n_msg,)),
@@ -314,26 +448,19 @@
             pltpu.SemaphoreType.DMA((2 * SUBS * nz,)),
         ],
         compiler_params=pltpu.CompilerParams(collective_id=0, has_side_effects=True, vmem_limit_bytes=40 * 2**20),
-    )(attn, w_o, hidden, gain)
+    )(attn, w_o, w_mate, hidden, gain)
 
 
 def solution(mesh):
     def local_step(hidden, w_q, w_k, w_v, w_o, q_norm_w, k_norm_w, post_norm_w, k_cache, v_cache, positions):
-        n_rows, width = hidden.shape
-        local_heads, head_dim = k_cache.shape[2], k_cache.shape[3]
-        q_local = jnp.dot(hidden, w_q, preferred_element_type=jnp.float32).astype(jnp.bfloat16).astype(jnp.float32)
-        k_local = jnp.dot(hidden, w_k, preferred_element_type=jnp.float32).astype(jnp.bfloat16).astype(jnp.float32)
-        v_local = jnp.dot(hidden, w_v, preferred_element_type=jnp.float32).astype(jnp.bfloat16)
-        energy = jnp.stack([jnp.sum(q_local * q_local, axis=-1), jnp.sum(k_local * k_local, axis=-1)])
-        energy = lax.psum(energy, 'tp')
-        inv_rms = lax.rsqrt(energy / width + NORM_EPS)
-        q_normed = (q_local * inv_rms[0][:, None] * q_norm_w).astype(jnp.bfloat16).reshape(n_rows, local_heads, head_dim)
-        k_normed = (k_local * inv_rms[1][:, None] * k_norm_w).astype(jnp.bfloat16).reshape(n_rows, local_heads, head_dim)
-        q_rot = apply_rope(q_normed, positions)
-        k_rot = apply_rope(k_normed, positions)
-        posb = jnp.broadcast_to(positions.astype(jnp.float32)[:, None], (n_rows, head_dim))
-        attn, k_new, v_new = attend_call(q_rot.reshape(n_rows, -1), k_rot.reshape(n_rows, -1), v_local, posb, positions, k_cache, v_cache)
-        hidden_out = finish_call(mesh.shape['tp'], attn, w_o, hidden, post_norm_w[None, :])
+        n_tp = mesh.shape["tp"]
+        slots, head_dim = k_cache.shape[1], k_cache.shape[3]
+        in_hbm = lambda x: pltpu.with_memory_space_constraint(x, pltpu.HBM)
+        hidden = in_hbm(hidden)
+        q_rot, k_rot, v_local, posb, w_mate = project_call(
+            n_tp, hidden, in_hbm(w_q), in_hbm(w_k), in_hbm(w_v), in_hbm(w_o), q_norm_w[None, :], k_norm_w[None, :], positions, slots, head_dim)
+        attn, k_new, v_new = attend_call(q_rot, k_rot, v_local, posb, positions, k_cache, v_cache)
+        hidden_out = finish_call(n_tp, attn, w_o, w_mate, hidden, post_norm_w[None, :])
         return hidden_out, k_new, v_new
 
     cache_spec = P('dp', None, 'tp', None)

time: 129 us -> 89.3 us (0.69)
  blocking collectives: 29 us -> 0 us
  Pallas kernels: 69.8 us -> 83.5 us
  local copies, waits for them, and re-layouts: 13.4 us -> 4.91 us
  other arithmetic: 7.85 us -> 0 us
  matrix products: 7.67 us -> 0 us
    psum x1 -> x0, blocking collectives: 29 us -> none  [local_step(): energy = lax.psum(energy, 'tp')]
    pallas_call x0 -> x1, Pallas kernels: none -> 18 us  [project_call(): pl.pallas_call(functools.partial(project_kernel, n_tp, slots, dim), name=...]
    dot_general x3 -> x0, matrix products: 7.67 us -> none  [the longest x1 4.25 us: local_step(): jnp.dot(hidden, w_v, preferred_element_type=jnp.float32)]
    unnamed x29 -> x17, local copies, waits for them, and re-layouts: 11.6 us -> 4.91 us
    pallas_call x1, Pallas kernels: 63.4 us -> 58.9 us  [finish_call(): pl.pallas_call(functools.partial(finish_kernel, n_tp), name='finish', out...]
    another operation x2 -> x0, other arithmetic: 2.51 us -> none
    convert_element_type x3 -> x0, other arithmetic: 2.08 us -> none  [the longest x1 1.15 us: local_step(): (k_local * inv_rms[1][:, None] * k_norm_w).astype(jnp.bfloat16)]
    cos x1 -> x0, other arithmetic: 1.81 us -> none  [apply_rope(): cos_tab = jnp.cos(angles)]
where the time goes in v3:
time: 89.3 us; the launch traced here: 89.1 us
  Pallas kernels  83.5 us (94%)
  local copies, waits for them, and re-layouts  4.91 us (5%)
    pallas_call x1, Pallas kernels, finish_call(): pl.pallas_call(functools.partial(finish_kernel, n_tp), name='finish', out...  58.9 us
    pallas_call x1, Pallas kernels, project_call(): pl.pallas_call(functools.partial(project_kernel, n_tp, slots, dim), name=...  18 us
    pallas_call x1, Pallas kernels, attend_call(): pl.pallas_call(functools.partial(attend_kernel, slots, heads), name='atte...  6.53 us
    unnamed x17, local copies, waits for them, and re-layouts  4.91 us

profile of v3, /device:TPU:21, one launch (start us, length us, event | category | flops | bytes accessed | tf_op | source)
XLA Modules:
  0.0 89.1 jit_solution(5120496015695251655)
XLA Ops:
  0.6 0.0 copy-start.3
  0.6 0.8 copy-done.3
  1.5 0.0 copy-start.5
  1.5 0.7 copy-done.5
  2.2 0.0 copy-start.6
  2.2 0.7 copy-done.6
  2.8 0.0 copy-start.7
  2.8 0.7 copy-done.7
  3.5 0.0 copy-start.1
  3.5 0.0 copy-start.2
  3.5 18.0 %project.1 = (bf16[512,256]{1,0:T(8,128)(2,1)S(1)}, bf16[512,256]{1,0:T(8,128)(2,1)S(1)}, bf16[512,256]{1,0:T(8,128)(2,1)S(1)}, f32[512,128]{1,0:T(8,128)S(1)}, bf16[256,4096]{1,0:T(8,128)(2,1)S(1)}) custom-call(s32[4,128]{1,0:T(4,128)S(1)} %bitcast.11, bf16[128,256]{1,0:T(8,128)(2,1)S(1)} %copy-done.3, f32[1,256]{1,0:T(1,128)S(1)} %bitcast.12, ...), custom_call_target="tpu_custom_call" | custom-call | flops 3221225472 | bytes 10485760 | tf_op jit(solution)/shard_map/project/pallas_call | solution.py:140
  21.6 0.0 copy-done.1
  21.6 0.0 copy-done.2
  21.6 0.0 copy-start
  21.6 0.0 copy-start.4
  21.6 6.5 %attend.1 = (bf16[512,256]{1,0:T(8,128)(2,1)S(1)}, bf16[16384,128]{1,0:T(8,128)(2,1)}, bf16[16384,128]{1,0:T(8,128)(2,1)}) custom-call(s32[512]{0:T(512)S(1)} %copy-done.5, bf16[512,256]{1,0:T(8,128)(2,1)S(1)} %get-tuple-element.11.q_ref, bf16[512,256]{1,0:T(8,128)(2,1)S(1)} %get-tuple-element.12.k_ref, bf16[512,256]{1,0:T(8,128)(2,1)S(1)} %get-tuple-element.13.v_ref, ...), custom_call_target="tpu_custom_call" | custom-call | tf_op jit(solution)/shard_map/attend/pallas_call | solution.py:227
  28.1 0.0 copy-done
  28.1 0.0 copy-done.4
  28.1 58.9 %finish.1 = bf16[512,4096]{1,0:T(8,128)(2,1)S(1)} custom-call(bf16[512,256]{1,0:T(8,128)(2,1)S(1)} %get-tuple-element.15.o_ref, bf16[256,4096]{1,0:T(8,128)(2,1)S(1)} %copy-done, bf16[256,4096]{1,0:T(8,128)(2,1)S(1)} %get-tuple-element.16.w_in, bf16[512,4096]{1,0:T(8,128)(2,1)} %hid_ref.3, f32[1,4096]{1,0:T(1,128)S(1)} %bitcast.10), custom_call_target="tpu_custom_call" | custom-call | tf_op jit(solution)/shard_map/finish/pallas_call | solution.py:428
  87.1 2.0 %copy.16 = bf16[512,4096]{1,0:T(8,128)(2,1)} copy(bf16[512,4096]{1,0:T(8,128)(2,1)S(1)} %finish.1) | data formatting | bytes 8388608
Async XLA Ops:
  0.6 0.8 copy-start.3
  1.5 0.7 copy-start.5
  2.2 0.7 copy-start.6
  2.8 0.7 copy-start.7
  3.5 18.0 %copy-start.1 = (bf16[512,16,2,128]{3,2,1,0:T(2,128)(2,1)S(1)}, bf16[512,16,2,128]{3,2,1,0:T(2,128)(2,1)}, u32[]{:S(2)}) copy-start(bf16[512,16,2,128]{3,2,1,0:T(2,128)(2,1)} %param.20) | copy-start | bytes 12582916
  3.5 18.0 %copy-start.2 = (bf16[512,16,2,128]{3,2,1,0:T(2,128)(2,1)S(1)}, bf16[512,16,2,128]{3,2,1,0:T(2,128)(2,1)}, u32[]{:S(2)}) copy-start(bf16[512,16,2,128]{3,2,1,0:T(2,128)(2,1)} %param.21) | copy-start | bytes 12582916
  21.6 6.6 %copy-start = (bf16[256,4096]{1,0:T(8,128)(2,1)S(1)}, bf16[256,4096]{1,0:T(8,128)(2,1)}, u32[]{:S(2)}) copy-start(bf16[256,4096]{1,0:T(8,128)(2,1)} %w_ref.1) | copy-start | bytes 6291460
  21.6 6.5 %copy-start.4 = (f32[4096]{0:T(1024)S(1)}, f32[4096]{0:T(1024)}, u32[]{:S(2)}) copy-start(f32[4096]{0:T(1024)} %param.19) | copy-start | bytes 49156

commit v4 on v3

--- a/solution.py
+++ b/solution.py
@@ -32,10 +32,10 @@
     return jnp.asarray(out, dtype=jnp.bfloat16)
 
 
-def project_kernel(n_tp, slots, dim, pos_ref, table_ref, qg_ref, kg_ref, hid_ref, wq_ref, wk_ref, wv_ref, wo_ref,
-                   q_ref, k_ref, v_ref, posb_ref, wo_in,
-                   hid, wqk, wv, acc, vacc, cosb, sinb, e_mine, e_in,
-                   in_sem, v_sem, e_send, e_recv, w_sem):
+def project_kernel(n_tp, slots, dim, pos_hbm, table_hbm, qg_hbm, kg_hbm, hid_ref, wq_ref, wk_ref, wv_ref, wo_ref, kc_ref, vc_ref,
+                   q_ref, k_ref, v_ref, posb_ref, wo_in, kc_out, vc_out,
+                   pos_ref, table_ref, qg_ref, kg_ref, hid, wqk, wv, acc, vacc, cosb, sinb, e_mine, e_in,
+                   in_sem, v_sem, e_send, e_recv, w_sem, s_sem, c_sem):
     t = lax.axis_index("tp")
     mate = t + 1 - 2 * lax.rem(t, 2)
     n_rows, width = hid_ref.shape
@@ -57,7 +57,10 @@
     for group in loads:
         for copy in group:
             copy.start()
-    for copy in v_loads:
+    small = [pltpu.make_async_copy(src, dst, s_sem.at[i]) for i, (src, dst) in enumerate(
+        ((pos_hbm, pos_ref), (table_hbm, table_ref), (qg_hbm, qg_ref), (kg_hbm, kg_ref)))]
+    caches = [pltpu.make_async_copy(src, dst, c_sem.at[i]) for i, (src, dst) in enumerate(((kc_ref, kc_out), (vc_ref, vc_out)))]
+    for copy in v_loads + small + caches:
         copy.start()
 
     w_copy = pltpu.make_async_remote_copy(wo_ref, wo_in, w_sem.at[0], w_sem.at[1], device_id={"tp": mate}, device_id_type=MESH)
@@ -101,6 +104,8 @@
             vacc[...] += part
         else:
             v_ref[...] = (vacc[...] + part).astype(jnp.bfloat16)
+    for copy in small:
+        copy.wait()
     lane = lax.broadcasted_iota(jnp.int32, (lanes, TABLE_ROWS), 1)
     which = jnp.where(lane < 3 * slots, lax.rem(lane, slots), -1).astype(jnp.float32)
     for b in range(blocks):
@@ -129,22 +134,31 @@
     for copy in sends:
         copy.wait_send()
     w_copy.wait()
-
-
-def project_call(n_tp, hidden, w_q, w_k, w_v, w_o, q_gain, k_gain, positions, slots, dim):
+    for copy in caches:
+        copy.wait()
+
+
+def project_call(n_tp, hidden, w_q, w_k, w_v, w_o, q_gain, k_gain, positions, k_cache, v_cache):
     n_rows, width = hidden.shape
     local = w_q.shape[1]
+    slots, dim = k_cache.shape[1], k_cache.shape[3]
     lanes = 128
+    flat = (k_cache.size // dim, dim)
+    in_hbm = lambda x: pltpu.with_memory_space_constraint(x, pltpu.HBM)
     cut = width // DEPTH_CUTS
     vmem, hbm = pl.BlockSpec(memory_space=pltpu.VMEM), pl.BlockSpec(memory_space=pltpu.HBM)
     return pl.pallas_call(
         functools.partial(project_kernel, n_tp, slots, dim),
         name="project",
         out_shape=[pltpu.VMEM((n_rows, local), jnp.bfloat16)] * 3
-        + [pltpu.VMEM((n_rows, lanes), jnp.float32), pltpu.VMEM(w_o.shape, jnp.bfloat16)],
-        in_specs=[vmem] * 4 + [hbm] * 5,
-        out_specs=[vmem] * 5,
+        + [pltpu.VMEM((n_rows, lanes), jnp.float32), pltpu.VMEM(w_o.shape, jnp.bfloat16)] + [pltpu.VMEM(flat, jnp.bfloat16)] * 2,
+        in_specs=[hbm] * 11,
+        out_specs=[vmem] * 7,
         scratch_shapes=[
+            pltpu.VMEM((n_rows // lanes, lanes), jnp.int32),
+            pltpu.VMEM((TABLE_ROWS, 2 * dim), jnp.bfloat16),
+            pltpu.VMEM((1, local), jnp.float32),
+            pltpu.VMEM((1, local), jnp.float32),
             pltpu.VMEM((DEPTH_CUTS, n_rows, cut), jnp.bfloat16),
             pltpu.VMEM((DEPTH_CUTS, cut, 2 * local), jnp.bfloat16),
             pltpu.VMEM((DEPTH_CUTS, cut, local), jnp.bfloat16),
@@ -159,13 +173,16 @@
             pltpu.SemaphoreType.DMA((n_tp,)),
             pltpu.SemaphoreType.DMA((n_tp,)),
             pltpu.SemaphoreType.DMA((2,)),
+            pltpu.SemaphoreType.DMA((4,)),
+            pltpu.SemaphoreType.DMA((2,)),
         ],
-        compiler_params=pltpu.CompilerParams(collective_id=1, has_side_effects=True, vmem_limit_bytes=24 * 2**20),
+        compiler_params=pltpu.CompilerParams(collective_id=1, has_side_effects=True, vmem_limit_bytes=32 * 2**20),
         cost_estimate=pl.CostEstimate(flops=6 * n_rows * width * local, bytes_accessed=2 * (n_rows * width + 3 * width * local), transcendentals=0),
-    )(positions.reshape(n_rows // lanes, lanes), rope_table(slots, dim), q_gain, k_gain, hidden, w_q, w_k, w_v, w_o)
-
-
-ROW_BLOCK = 64
+    )(*map(in_hbm, (positions.reshape(n_rows // lanes, lanes), rope_table(slots, dim), q_gain, k_gain, hidden, w_q, w_k, w_v, w_o,
+                    k_cache.reshape(flat), v_cache.reshape(flat))))
+
+
+ROW_BLOCK = 128
 GROUP = 8
 
 
@@ -217,8 +234,8 @@
             o_ref[g * GROUP:(g + 1) * GROUP, h * dim:(h + 1) * dim] = o[h * GROUP:(h + 1) * GROUP]
 
 
-def attend_call(q, k, v, posb, positions, k_cache, v_cache):
-    n_rows, slots, heads, dim = k_cache.shape
+def attend_call(q, k, v, posb, positions, k_cache, v_cache, cache_shape):
+    n_rows, slots, heads, dim = cache_shape
     lines = slots * heads
     flat = (n_rows * lines, dim)
     block = ROW_BLOCK
@@ -237,16 +254,17 @@
             scratch_shapes=[pltpu.VMEM((block, heads * dim), jnp.float32), pltpu.VMEM((block, heads * dim), jnp.float32)],
         ),
         compiler_params=pltpu.CompilerParams(vmem_limit_bytes=24 * 2**20),
-    )(positions, q, k, v, posb, k_cache.reshape(flat), v_cache.reshape(flat))
-    return o, k_new.reshape(k_cache.shape), v_new.reshape(v_cache.shape)
+    )(positions, q, k, v, posb, k_cache, v_cache)
+    return o, k_new.reshape(cache_shape), v_new.reshape(cache_shape)
 
 
 SUBS = 2
-LAG = 2
+LAG = 0
+SHARE_TILE = 2048
 
 
 def finish_kernel(n_tp, o_ref, w_ref, w_in, hid_ref, gain_ref, out_ref,
-                  o_in, hid, share, rs_in, rs_out,
+                  o_in, lhs, lhs_in, hid, share, rs_in, rs_out,
                   x_send, x_recv, h_sem, rs_send, rs_recv, ag_send, ag_recv, d2d_send, d2d_recv):
     nz = n_tp // 2
     t = lax.axis_index("tp")
@@ -275,21 +293,26 @@
         o_ref.at[pl.ds(pl.multiple_of((1 - k) * half_rows, half_rows), half_rows), :], o_in,
         x_send, x_recv, device_id={"tp": mate}, device_id_type=MESH)
     o_copy.start()
+
+    order = sorted(range(nz), key=lambda j: -min(j, nz - j))
+    place = {j: i for i, j in enumerate(order)}
+    for j in range(nz):
+        at = slice(place[j] * rows, (place[j] + 1) * rows)
+        lhs[at, :] = o_ref[pl.ds(pl.multiple_of(k * half_rows + chunk_of(j) * rows, rows), rows), :]
     o_copy.wait_recv()
-
-    tile = min(1024, width)
-
-    def make_share(j):
-        own = o_ref[pl.ds(pl.multiple_of(k * half_rows + chunk_of(j) * rows, rows), rows), :]
-        other = o_in[pl.ds(pl.multiple_of(chunk_of(j) * rows, rows), rows), :]
-
+    for j in range(nz):
+        at = slice(place[j] * rows, (place[j] + 1) * rows)
+        lhs_in[at, :] = o_in[pl.ds(pl.multiple_of(chunk_of(j) * rows, rows), rows), :]
+
+    def make_shares(first, last):
         def one(c, carry):
-            at = pl.ds(pl.multiple_of(c * tile, tile), tile)
-            share[j % nz, :, at] = (jnp.dot(own, w_ref[:, at], preferred_element_type=jnp.float32)
-                                    + jnp.dot(other, w_in[:, at], preferred_element_type=jnp.float32))
+            at = pl.ds(pl.multiple_of(c * SHARE_TILE, SHARE_TILE), SHARE_TILE)
+            share[first * rows:last * rows, at] = (
+                jnp.dot(lhs[first * rows:last * rows, :], w_ref[:, at], preferred_element_type=jnp.float32)
+                + jnp.dot(lhs_in[first * rows:last * rows, :], w_in[:, at], preferred_element_type=jnp.float32))
             return carry
 
-        lax.fori_loop(0, width // tile, one, 0)
+        lax.fori_loop(0, width // SHARE_TILE, one, 0)
 
     def hops(d, c):
         return far if c == long_half[d] else far - 1
@@ -307,7 +330,7 @@
             rs_out.at[i], rs_in.at[i], rs_send.at[i], rs_recv.at[i], device_id={"tp": target[d]}, device_id_type=MESH)
 
     def piece(j, c, s):
-        return share[j % nz, s * sub:(s + 1) * sub, c * half:(c + 1) * half]
+        return share[place[j % nz] * rows + s * sub:place[j % nz] * rows + (s + 1) * sub, c * half:(c + 1) * half]
 
     def rs_step(d, c, h, s):
         ahead = hops(d, c) - h
@@ -351,12 +374,12 @@
                 last = hops(d, c) - 1
                 rs_message(d, c, last, s).wait_recv()
                 acc = acc + rs_in[slots[d, c, last, s]].astype(jnp.float32)
-            share[0, s * sub:(s + 1) * sub, c * half:(c + 1) * half] = acc
+            share[place[0] * rows + s * sub:place[0] * rows + (s + 1) * sub, c * half:(c + 1) * half] = acc
             total.append(jnp.sum(acc * acc, axis=-1, keepdims=True))
         inv = lax.rsqrt((total[0] + total[1]) / width + NORM_EPS)
         for c in range(2):
             at = slice(c * half, (c + 1) * half)
-            normed = share[0, s * sub:(s + 1) * sub, at] * inv * gain_ref[:, at]
+            normed = piece(0, c, s) * inv * gain_ref[:, at]
             out_ref[pl.ds(out_row(0, s), sub), at] = (hid[s * sub:(s + 1) * sub, at].astype(jnp.float32) + normed).astype(jnp.bfloat16)
         for d in range(2):
             for c in (long_half[d], 1 - long_half[d]):
@@ -379,17 +402,7 @@
                 for d in range(2):
                     c = long_half[d] if longer else 1 - long_half[d]
                     if g < hops(d, c):
-                        if g == 0 and s == 0:
-                            j = hops(d, c) if d == 0 else -hops(d, c)
-                            if j % nz not in made:
-                                make_share(j)
-                                made.add(j % nz)
                         rs_step(d, c, g, s)
-            if g == 0 and s == 0:
-                for j in sorted(range(nz), key=lambda j: -min(j, nz - j)):
-                    if j not in made:
-                        make_share(j)
-                        made.add(j)
         elif g == far:
             if s == 0:
                 hid_copy.wait()
@@ -397,9 +410,11 @@
         else:
             ag_step(g - far, s)
 
-    made = set()
+    make_shares(0, 3)
     last_stage = 2 * far
     for slot in range(last_stage + 1 + LAG * (SUBS - 1)):
+        if slot == 1:
+            make_shares(3, nz)
         for s in range(SUBS):
             g = slot - LAG * s
             if 0 <= g <= last_stage:
@@ -433,8 +448,10 @@
         out_specs=vmem,
         scratch_shapes=[
             pltpu.VMEM((half_rows, depth), jnp.bfloat16),
+            pltpu.VMEM((half_rows, depth), jnp.bfloat16),
+            pltpu.VMEM((half_rows, depth), jnp.bfloat16),
             pltpu.VMEM((rows, width), jnp.bfloat16),
-            pltpu.VMEM((nz, rows, width), jnp.float32),
+            pltpu.VMEM((half_rows, width), jnp.float32),
             pltpu.VMEM((n_msg, sub, width // 2), jnp.bfloat16),
             pltpu.VMEM((n_msg, sub, width // 2), jnp.bfloat16),
             pltpu.SemaphoreType.DMA,
@@ -448,18 +465,15 @@
             pltpu.SemaphoreType.DMA((2 * SUBS * nz,)),
         ],
         compiler_params=pltpu.CompilerParams(collective_id=0, has_side_effects=True, vmem_limit_bytes=40 * 2**20),
-    )(attn, w_o, w_mate, hidden, gain)
+    )(attn, w_o, w_mate, pltpu.with_memory_space_constraint(hidden, pltpu.HBM), gain)
 
 
 def solution(mesh):
     def local_step(hidden, w_q, w_k, w_v, w_o, q_norm_w, k_norm_w, post_norm_w, k_cache, v_cache, positions):
         n_tp = mesh.shape["tp"]
-        slots, head_dim = k_cache.shape[1], k_cache.shape[3]
-        in_hbm = lambda x: pltpu.with_memory_space_constraint(x, pltpu.HBM)
-        hidden = in_hbm(hidden)
-        q_rot, k_rot, v_local, posb, w_mate = project_call(
-            n_tp, hidden, in_hbm(w_q), in_hbm(w_k), in_hbm(w_v), in_hbm(w_o), q_norm_w[None, :], k_norm_w[None, :], positions, slots, head_dim)
-        attn, k_new, v_new = attend_call(q_rot, k_rot, v_local, posb, positions, k_cache, v_cache)
+        q_rot, k_rot, v_local, posb, w_mate, k_near, v_near = project_call(
+            n_tp, hidden, w_q, w_k, w_v, w_o, q_norm_w[None, :], k_norm_w[None, :], positions, k_cache, v_cache)
+        attn, k_new, v_new = attend_call(q_rot, k_rot, v_local, posb, positions, k_near, v_near, k_cache.shape)
         hidden_out = finish_call(n_tp, attn, w_o, w_mate, hidden, post_norm_w[None, :])
         return hidden_out, k_new, v_new
 

time: 89.3 us -> 77.4 us (0.87)
  Pallas kernels: 83.5 us -> 74.6 us
  local copies, waits for them, and re-layouts: 4.91 us -> 2.03 us
    pallas_call x1, Pallas kernels: 58.9 us -> 50.4 us  [finish_call(): pl.pallas_call(functools.partial(finish_kernel, n_tp), name='finish', out...]
    unnamed x17 -> x7, local copies, waits for them, and re-layouts: 4.91 us -> 2.03 us
where the time goes in v4:
time: 77.4 us; the launch traced here: 77.3 us
  Pallas kernels  74.6 us (96%)
  local copies, waits for them, and re-layouts  2.03 us (3%)
    pallas_call x1, Pallas kernels, finish_call(): pl.pallas_call(functools.partial(finish_kernel, n_tp), name='finish', out...  50.4 us
    pallas_call x1, Pallas kernels, project_call(): pl.pallas_call(functools.partial(project_kernel, n_tp, slots, dim), name=...  18.2 us
    pallas_call x1, Pallas kernels, attend_call(): pl.pallas_call(functools.partial(attend_kernel, slots, heads), name='atte...  5.99 us
    unnamed x7, local copies, waits for them, and re-layouts  2.03 us

profile of v4, /device:TPU:21, one launch (start us, length us, event | category | flops | bytes accessed | tf_op | source)
XLA Modules:
  0.0 77.3 jit_solution(12951613814277298874)
XLA Ops:
  0.6 0.0 copy-start.2
  0.6 18.2 %project.1 = (bf16[512,256]{1,0:T(8,128)(2,1)S(1)}, bf16[512,256]{1,0:T(8,128)(2,1)S(1)}, bf16[512,256]{1,0:T(8,128)(2,1)S(1)}, f32[512,128]{1,0:T(8,128)S(1)}, ...) custom-call(s32[4,128]{1,0:T(4,128)} %bitcast.9, ...), custom_call_target="tpu_custom_call" | custom-call | flops 3221225472 | bytes 10485760 | tf_op jit(solution)/shard_map/project/pallas_call | solution.py:150
  18.9 0.0 copy-done.2
  18.9 0.0 copy-start
  18.9 0.0 copy-start.1
  18.9 6.0 %attend.1 = (bf16[512,256]{1,0:T(8,128)(2,1)S(1)}, bf16[16384,128]{1,0:T(8,128)(2,1)}, bf16[16384,128]{1,0:T(8,128)(2,1)}) custom-call(s32[512]{0:T(512)S(1)} %copy-done.2, bf16[512,256]{1,0:T(8,128)(2,1)S(1)} %get-tuple-element.13.q_ref, bf16[512,256]{1,0:T(8,128)(2,1)S(1)} %get-tuple-element.14.k_ref, bf16[512,256]{1,0:T(8,128)(2,1)S(1)} %get-tuple-element.15.v_ref, ...), custom_call_target="tpu_custom_call" | custom-call | tf_op jit(solution)/shard_map/attend/pallas_call | solution.py:244
  24.9 0.0 copy-done
  24.9 0.0 copy-done.1
  24.9 50.4 %finish.1 = bf16[512,4096]{1,0:T(8,128)(2,1)S(1)} custom-call(bf16[512,256]{1,0:T(8,128)(2,1)S(1)} %get-tuple-element.19.o_ref, bf16[256,4096]{1,0:T(8,128)(2,1)S(1)} %copy-done, bf16[256,4096]{1,0:T(8,128)(2,1)S(1)} %get-tuple-element.20.w_in, bf16[512,4096]{1,0:T(8,128)(2,1)} %hid_ref.3, f32[1,4096]{1,0:T(1,128)S(1)} %bitcast.8), custom_call_target="tpu_custom_call" | custom-call | tf_op jit(solution)/shard_map/finish/pallas_call | solution.py:443
  75.3 2.0 %copy.16 = bf16[512,4096]{1,0:T(8,128)(2,1)} copy(bf16[512,4096]{1,0:T(8,128)(2,1)S(1)} %finish.1) | data formatting | bytes 8388608
Async XLA Ops:
  0.6 18.3 %copy-start.2 = (s32[512]{0:T(512)S(1)}, s32[512]{0:T(512)}, u32[]{:S(2)}) copy-start(s32[512]{0:T(512)} %pos_ref.1) | copy-start | bytes 6148
  18.9 6.0 %copy-start = (bf16[256,4096]{1,0:T(8,128)(2,1)S(1)}, bf16[256,4096]{1,0:T(8,128)(2,1)}, u32[]{:S(2)}) copy-start(bf16[256,4096]{1,0:T(8,128)(2,1)} %w_ref.1) | copy-start | bytes 6291460
  18.9 6.0 %copy-start.1 = (f32[4096]{0:T(1024)S(1)}, f32[4096]{0:T(1024)}, u32[]{:S(2)}) copy-start(f32[4096]{0:T(1024)} %param.19) | copy-start | bytes 49156

commit v5 on v4

--- a/solution.py
+++ b/solution.py
@@ -32,9 +32,32 @@
     return jnp.asarray(out, dtype=jnp.bfloat16)
 
 
+def inserter(slots, heads, dim):
+    assert heads == 2
+    part_lines = slots * heads // 2
+    line = lax.broadcasted_iota(jnp.int32, (part_lines, dim), 0)
+    first = lax.rem(line, heads) == 0
+    slot_of = [(line // heads + part * (slots // 2)).astype(jnp.float32).astype(jnp.bfloat16) for part in range(2)]
+
+    def insert(posb_ref, fresh_ref, start, count, old, new):
+        spots = [pl.ds(pl.multiple_of((start + r) * 2 * part_lines, 2 * part_lines) + part * part_lines, part_lines)
+                 for r in range(count) for part in range(2)]
+        before = [old[at, :] for at in spots]
+        for r in range(count):
+            row = pl.ds(start + r, 1)
+            p = jnp.broadcast_to(posb_ref[row, :], (part_lines, dim)).astype(jnp.bfloat16)
+            h0 = jnp.broadcast_to(fresh_ref[0, row, :], (part_lines, dim))
+            h1 = jnp.broadcast_to(fresh_ref[1, row, :], (part_lines, dim))
+            fresh = jnp.where(first, h0, h1).astype(jnp.bfloat16)
+            for part in range(2):
+                new[spots[2 * r + part], :] = jnp.where(slot_of[part] == p, fresh, before[2 * r + part])
+
+    return insert
+
+
 def project_kernel(n_tp, slots, dim, pos_hbm, table_hbm, qg_hbm, kg_hbm, hid_ref, wq_ref, wk_ref, wv_ref, wo_ref, kc_ref, vc_ref,
-                   q_ref, k_ref, v_ref, posb_ref, wo_in, kc_out, vc_out,
-                   pos_ref, table_ref, qg_ref, kg_ref, hid, wqk, wv, acc, vacc, cosb, sinb, e_mine, e_in,
+                   q_ref, k_ref, posb_ref, wo_own, wo_in, kc_out, vc_out,
+                   pos_ref, table_ref, qg_ref, kg_ref, hid, wqk, wv, vc_in, acc, vacc, cosb, sinb, e_mine, e_in,
                    in_sem, v_sem, e_send, e_recv, w_sem, s_sem, c_sem):
     t = lax.axis_index("tp")
     mate = t + 1 - 2 * lax.rem(t, 2)
@@ -59,11 +82,11 @@
             copy.start()
     small = [pltpu.make_async_copy(src, dst, s_sem.at[i]) for i, (src, dst) in enumerate(
         ((pos_hbm, pos_ref), (table_hbm, table_ref), (qg_hbm, qg_ref), (kg_hbm, kg_ref)))]
-    caches = [pltpu.make_async_copy(src, dst, c_sem.at[i]) for i, (src, dst) in enumerate(((kc_ref, kc_out), (vc_ref, vc_out)))]
-    for copy in v_loads + small + caches:
+    caches = [pltpu.make_async_copy(src, dst, c_sem.at[i]) for i, (src, dst) in enumerate(((kc_ref, kc_out), (vc_ref, vc_in), (wo_ref, wo_own)))]
+    for copy in v_loads + small + [caches[2], caches[1], caches[0]]:
         copy.start()
 
-    w_copy = pltpu.make_async_remote_copy(wo_ref, wo_in, w_sem.at[0], w_sem.at[1], device_id={"tp": mate}, device_id_type=MESH)
+    w_copy = pltpu.make_async_remote_copy(wo_own, wo_in, w_sem.at[0], w_sem.at[1], device_id={"tp": mate}, device_id_type=MESH)
     for c in range(DEPTH_CUTS):
         for copy in loads[c]:
             copy.wait()
@@ -72,9 +95,6 @@
             acc[...] = part
         else:
             acc[...] += part
-        if c == DEPTH_CUTS - 2:
-            pl.semaphore_wait(barrier, n_tp - 1)
-            w_copy.start()
 
     lanes = e_mine.shape[1]
     blocks = n_rows // lanes
@@ -89,21 +109,23 @@
                   + lax.dot_general(ones, low, nt, preferred_element_type=jnp.float32))
         for b in range(blocks):
             e_mine[i * blocks + b:i * blocks + b + 1, :] = energy[0:1, b * lanes:(b + 1) * lanes]
+    pl.semaphore_wait(barrier, n_tp - 1)
     sends = [pltpu.make_async_remote_copy(
         e_mine, e_in.at[off], e_send.at[off], e_recv.at[off],
         device_id={"tp": lax.rem(t + off, n_tp)}, device_id_type=MESH) for off in range(1, n_tp)]
     for copy in sends:
         copy.start()
+    caches[2].wait()
+    w_copy.start()
 
     for c in range(DEPTH_CUTS):
         v_loads[c].wait()
         part = jnp.dot(hid[c], wv[c], preferred_element_type=jnp.float32)
-        if c == 0:
-            vacc[...] = part
-        elif c < DEPTH_CUTS - 1:
-            vacc[...] += part
-        else:
-            v_ref[...] = (vacc[...] + part).astype(jnp.bfloat16)
+        for h in range(heads):
+            if c == 0:
+                vacc[h] = part[:, h * dim:(h + 1) * dim]
+            else:
+                vacc[h] += part[:, h * dim:(h + 1) * dim]
     for copy in small:
         copy.wait()
     lane = lax.broadcasted_iota(jnp.int32, (lanes, TABLE_ROWS), 1)
@@ -116,6 +138,14 @@
         factors = jnp.dot(hot, table_ref[...], preferred_element_type=jnp.float32)
         cosb[at, :] = factors[:, :dim]
         sinb[at, :] = factors[:, dim:]
+    caches[1].wait()
+    insert = inserter(slots, heads, dim)
+
+    def insert_rows(i, carry):
+        insert(posb_ref, vacc, i * INSERT_UNROLL, INSERT_UNROLL, vc_in, vc_out)
+        return carry
+
+    lax.fori_loop(0, n_rows // INSERT_UNROLL, insert_rows, 0)
 
     total = e_mine[...]
     for i, copy in enumerate(sends):
@@ -130,12 +160,15 @@
                 cols = slice(h * dim, (h + 1) * dim)
                 x = acc[at, i * local + h * dim:i * local + (h + 1) * dim].astype(jnp.bfloat16).astype(jnp.float32)
                 x = (x * scale * gain[:, cols]).astype(jnp.bfloat16).astype(jnp.float32)
-                out[at, cols] = (x * cosb[at, :] + pltpu.roll(x, dim // 2, 1) * sinb[at, :]).astype(jnp.bfloat16)
+                x = (x * cosb[at, :] + pltpu.roll(x, dim // 2, 1) * sinb[at, :]).astype(jnp.bfloat16)
+                if i == 0:
+                    out[at, cols] = x
+                else:
+                    out[h, at, :] = x.astype(jnp.float32)
     for copy in sends:
         copy.wait_send()
     w_copy.wait()
-    for copy in caches:
-        copy.wait()
+    caches[0].wait()
 
 
 def project_call(n_tp, hidden, w_q, w_k, w_v, w_o, q_gain, k_gain, positions, k_cache, v_cache):
@@ -150,8 +183,8 @@
     return pl.pallas_call(
         functools.partial(project_kernel, n_tp, slots, dim),
         name="project",
-        out_shape=[pltpu.VMEM((n_rows, local), jnp.bfloat16)] * 3
-        + [pltpu.VMEM((n_rows, lanes), jnp.float32), pltpu.VMEM(w_o.shape, jnp.bfloat16)] + [pltpu.VMEM(flat, jnp.bfloat16)] * 2,
+        out_shape=[pltpu.VMEM((n_rows, local), jnp.bfloat16), pltpu.VMEM((local // dim, n_rows, dim), jnp.float32)]
+        + [pltpu.VMEM((n_rows, lanes), jnp.float32), pltpu.VMEM(w_o.shape, jnp.bfloat16), pltpu.VMEM(w_o.shape, jnp.bfloat16)] + [pltpu.VMEM(flat, jnp.bfloat16)] * 2,
         in_specs=[hbm] * 11,
         out_specs=[vmem] * 7,
         scratch_shapes=[
@@ -162,8 +195,9 @@
             pltpu.VMEM((DEPTH_CUTS, n_rows, cut), jnp.bfloat16),
             pltpu.VMEM((DEPTH_CUTS, cut, 2 * local), jnp.bfloat16),
             pltpu.VMEM((DEPTH_CUTS, cut, local), jnp.bfloat16),
+            pltpu.VMEM(flat, jnp.bfloat16),
             pltpu.VMEM((n_rows, 2 * local), jnp.float32),
-            pltpu.VMEM((n_rows, local), jnp.float32),
+            pltpu.VMEM((local // dim, n_rows, dim), jnp.float32),
             pltpu.VMEM((n_rows, dim), jnp.float32),
             pltpu.VMEM((n_rows, dim), jnp.float32),
             pltpu.VMEM((2 * n_rows // lanes, lanes), jnp.float32),
@@ -174,88 +208,88 @@
             pltpu.SemaphoreType.DMA((n_tp,)),
             pltpu.SemaphoreType.DMA((2,)),
             pltpu.SemaphoreType.DMA((4,)),
-            pltpu.SemaphoreType.DMA((2,)),
+            pltpu.SemaphoreType.DMA((3,)),
         ],
-        compiler_params=pltpu.CompilerParams(collective_id=1, has_side_effects=True, vmem_limit_bytes=32 * 2**20),
+        compiler_params=pltpu.CompilerParams(collective_id=1, has_side_effects=True, vmem_limit_bytes=40 * 2**20),
         cost_estimate=pl.CostEstimate(flops=6 * n_rows * width * local, bytes_accessed=2 * (n_rows * width + 3 * width * local), transcendentals=0),
     )(*map(in_hbm, (positions.reshape(n_rows // lanes, lanes), rope_table(slots, dim), q_gain, k_gain, hidden, w_q, w_k, w_v, w_o,
                     k_cache.reshape(flat), v_cache.reshape(flat))))
 
 
-ROW_BLOCK = 128
+ROW_BLOCK = 256
+INSERT_UNROLL = 16
 GROUP = 8
 
 
-def attend_kernel(slots, heads, pos_ref, q_ref, k_ref, v_ref, posb_ref, kc_ref, vc_ref, o_ref, kn_ref, vn_ref, kf, vf):
-    block = q_ref.shape[0]
+def attend_kernel(slots, heads, q_ref, k_ref, posb_ref, kc_ref, vn_ref, o_ref, k_out, v_out, kn, k_sem, v_sem):
+    n_rows = q_ref.shape[0]
     dim = q_ref.shape[1] // heads
     lines = slots * heads
-    step = pl.program_id(0)
-    kf[...] = k_ref[...].astype(jnp.float32)
-    vf[...] = v_ref[...].astype(jnp.float32)
-    line = lax.broadcasted_iota(jnp.int32, (lines // 2, dim), 0)
-    first = lax.rem(line, heads) == 0
-    slot_of = [(line // heads + part * (slots // 2)).astype(jnp.float32).astype(jnp.bfloat16) for part in range(2)]
-
-    def insert(r):
-        p = jnp.full((lines // 2, dim), pos_ref[step * block + r].astype(jnp.float32)).astype(jnp.bfloat16)
-        for src, old, new in ((kf, kc_ref, kn_ref), (vf, vc_ref, vn_ref)):
-            h0 = jnp.broadcast_to(src[pl.ds(r, 1), 0:dim], (lines // 2, dim))
-            h1 = jnp.broadcast_to(src[pl.ds(r, 1), dim:2 * dim], (lines // 2, dim))
-            fresh = jnp.where(first, h0, h1).astype(jnp.bfloat16)
-            for part in range(2):
-                at = pl.ds(r * lines + part * (lines // 2), lines // 2)
-                new[at, :] = jnp.where(slot_of[part] == p, fresh, old[at, :])
-
-    for r in range(block):
-        insert(r)
-
+    block = ROW_BLOCK
+    v_copy = pltpu.make_async_copy(vn_ref, v_out, v_sem)
+    v_copy.start()
+    insert = inserter(slots, heads, dim)
     n_groups = block // GROUP
     wide = GROUP * lines
     m = lax.broadcasted_iota(jnp.int32, (heads * GROUP, wide), 0)
     n = lax.broadcasted_iota(jnp.int32, (heads * GROUP, wide), 1)
     own = (lax.rem(m, GROUP) == n // lines) & (m // GROUP == lax.rem(n, heads))
     slot = jnp.where(own, (lax.rem(n, lines) // heads).astype(jnp.float32), 1e9)
-    scores = []
-    for g in range(n_groups):
-        rows = slice(g * GROUP, (g + 1) * GROUP)
-        q = jnp.concatenate([q_ref[rows, h * dim:(h + 1) * dim] for h in range(heads)], axis=0)
-        keys = kn_ref[g * wide:(g + 1) * wide, :]
-        s = lax.dot_general(q, keys, (((1,), (1,)), ((), ())), preferred_element_type=jnp.float32) * dim ** -0.5
-        at = jnp.concatenate([posb_ref[rows, :]] * heads, axis=0)
-        at = jnp.concatenate([at] * (wide // at.shape[1]), axis=1)
-        scores.append(jnp.where(slot <= at, s, -1e30))
-    for g in range(n_groups):
-        s = scores[g]
-        e = jnp.exp(s - jnp.max(s, axis=-1, keepdims=True))
-        probs = (e / jnp.sum(e, axis=-1, keepdims=True)).astype(jnp.bfloat16)
-        o = jnp.dot(probs, vn_ref[g * wide:(g + 1) * wide, :], preferred_element_type=jnp.float32).astype(jnp.bfloat16)
-        for h in range(heads):
-            o_ref[g * GROUP:(g + 1) * GROUP, h * dim:(h + 1) * dim] = o[h * GROUP:(h + 1) * GROUP]
-
-
-def attend_call(q, k, v, posb, positions, k_cache, v_cache, cache_shape):
+
+    def k_copy(i):
+        at = pl.ds(pl.multiple_of(i * block * lines, block * lines), block * lines)
+        return pltpu.make_async_copy(kn.at[at, :], k_out.at[at, :], k_sem.at[i])
+
+    def fill(i, carry):
+        for r in range(0, block, INSERT_UNROLL):
+            insert(posb_ref, k_ref, i * block + r, INSERT_UNROLL, kc_ref, kn)
+        k_copy(i).start()
+        return carry
+
+    lax.fori_loop(0, n_rows // block, fill, 0)
+
+    def one(i, carry):
+        scores = []
+        for g in range(n_groups):
+            rows = pl.ds(pl.multiple_of(i * block + g * GROUP, GROUP), GROUP)
+            keys = kn[pl.ds(pl.multiple_of((i * n_groups + g) * wide, wide), wide), :]
+            q = jnp.concatenate([q_ref[rows, h * dim:(h + 1) * dim] for h in range(heads)], axis=0)
+            s = lax.dot_general(q, keys, (((1,), (1,)), ((), ())), preferred_element_type=jnp.float32) * dim ** -0.5
+            at = jnp.concatenate([posb_ref[rows, :]] * heads, axis=0)
+            at = jnp.concatenate([at] * (wide // at.shape[1]), axis=1)
+            scores.append(jnp.where(slot <= at, s, -1e30))
+        for g in range(n_groups):
+            rows = pl.ds(pl.multiple_of(i * block + g * GROUP, GROUP), GROUP)
+            values = vn_ref[pl.ds(pl.multiple_of((i * n_groups + g) * wide, wide), wide), :]
+            s = scores[g]
+            e = jnp.exp(s - jnp.max(s, axis=-1, keepdims=True))
+            probs = (e / jnp.sum(e, axis=-1, keepdims=True)).astype(jnp.bfloat16)
+            o = jnp.dot(probs, values, preferred_element_type=jnp.float32).astype(jnp.bfloat16)
+            for h in range(heads):
+                o_ref[rows, h * dim:(h + 1) * dim] = o[h * GROUP:(h + 1) * GROUP]
+        return carry
+
+    lax.fori_loop(0, n_rows // block, one, 0)
+    for i in range(n_rows // block):
+        k_copy(i).wait()
+    v_copy.wait()
+
+
+def attend_call(q, k, posb, k_cache, v_new, cache_shape):
     n_rows, slots, heads, dim = cache_shape
-    lines = slots * heads
-    flat = (n_rows * lines, dim)
-    block = ROW_BLOCK
-    row_spec = pl.BlockSpec((block, heads * dim), lambda i, pos: (i, 0))
-    cache_spec = pl.BlockSpec((block * lines, dim), lambda i, pos: (i, 0))
-    o, k_new, v_new = pl.pallas_call(
+    flat = (n_rows * slots * heads, dim)
+    vmem, hbm = pl.BlockSpec(memory_space=pltpu.VMEM), pl.BlockSpec(memory_space=pltpu.HBM)
+    o, k_out, v_out = pl.pallas_call(
         functools.partial(attend_kernel, slots, heads),
         name="attend",
-        out_shape=[jax.ShapeDtypeStruct((n_rows, heads * dim), jnp.bfloat16),
-                   jax.ShapeDtypeStruct(flat, jnp.bfloat16), jax.ShapeDtypeStruct(flat, jnp.bfloat16)],
-        grid_spec=pltpu.PrefetchScalarGridSpec(
-            num_scalar_prefetch=1,
-            grid=(n_rows // block,),
-            in_specs=[row_spec, row_spec, row_spec, pl.BlockSpec((block, dim), lambda i, pos: (i, 0)), cache_spec, cache_spec],
-            out_specs=[row_spec, cache_spec, cache_spec],
-            scratch_shapes=[pltpu.VMEM((block, heads * dim), jnp.float32), pltpu.VMEM((block, heads * dim), jnp.float32)],
-        ),
+        out_shape=[pltpu.VMEM((n_rows, heads * dim), jnp.bfloat16),
+                   pltpu.HBM(flat, jnp.bfloat16), pltpu.HBM(flat, jnp.bfloat16)],
+        in_specs=[vmem] * 5,
+        out_specs=[vmem, hbm, hbm],
+        scratch_shapes=[pltpu.VMEM(flat, jnp.bfloat16), pltpu.SemaphoreType.DMA((n_rows // ROW_BLOCK,)), pltpu.SemaphoreType.DMA],
         compiler_params=pltpu.CompilerParams(vmem_limit_bytes=24 * 2**20),
-    )(positions, q, k, v, posb, k_cache, v_cache)
-    return o, k_new.reshape(cache_shape), v_new.reshape(cache_shape)
+    )(q, k, posb, k_cache, v_new)
+    return o, k_out.reshape(cache_shape), v_out.reshape(cache_shape)
 
 
 SUBS = 2
@@ -299,20 +333,24 @@
     for j in range(nz):
         at = slice(place[j] * rows, (place[j] + 1) * rows)
         lhs[at, :] = o_ref[pl.ds(pl.multiple_of(k * half_rows + chunk_of(j) * rows, rows), rows), :]
+
+    def add_shares(first, last, lhs_ref, weight, fresh):
+        def one(c, carry):
+            at = pl.ds(pl.multiple_of(c * SHARE_TILE, SHARE_TILE), SHARE_TILE)
+            part = jnp.dot(lhs_ref[first * rows:last * rows, :], weight[:, at], preferred_element_type=jnp.float32)
+            if fresh:
+                share[first * rows:last * rows, at] = part
+            else:
+                share[first * rows:last * rows, at] += part
+            return carry
+
+        lax.fori_loop(0, width // SHARE_TILE, one, 0)
+
+    add_shares(0, nz, lhs, w_ref, True)
     o_copy.wait_recv()
     for j in range(nz):
         at = slice(place[j] * rows, (place[j] + 1) * rows)
         lhs_in[at, :] = o_in[pl.ds(pl.multiple_of(chunk_of(j) * rows, rows), rows), :]
-
-    def make_shares(first, last):
-        def one(c, carry):
-            at = pl.ds(pl.multiple_of(c * SHARE_TILE, SHARE_TILE), SHARE_TILE)
-            share[first * rows:last * rows, at] = (
-                jnp.dot(lhs[first * rows:last * rows, :], w_ref[:, at], preferred_element_type=jnp.float32)
-                + jnp.dot(lhs_in[first * rows:last * rows, :], w_in[:, at], preferred_element_type=jnp.float32))
-            return carry
-
-        lax.fori_loop(0, width // SHARE_TILE, one, 0)
 
     def hops(d, c):
         return far if c == long_half[d] else far - 1
@@ -410,11 +448,11 @@
         else:
             ag_step(g - far, s)
 
-    make_shares(0, 3)
+    add_shares(0, 3, lhs_in, w_in, False)
     last_stage = 2 * far
     for slot in range(last_stage + 1 + LAG * (SUBS - 1)):
         if slot == 1:
-            make_shares(3, nz)
+            add_shares(3, nz, lhs_in, w_in, False)
         for s in range(SUBS):
             g = slot - LAG * s
             if 0 <= g <= last_stage:
@@ -432,9 +470,9 @@
         copy.wait_recv()
 
 
-def finish_call(n_tp, attn, w_o, w_mate, hidden, gain):
+def finish_call(n_tp, attn, w_own, w_mate, hidden, gain):
     n_rows, width = hidden.shape
-    depth = w_o.shape[0]
+    depth = w_own.shape[0]
     nz = n_tp // 2
     half_rows, rows = n_rows // 2, n_rows // n_tp
     sub = rows // SUBS
@@ -465,16 +503,16 @@
             pltpu.SemaphoreType.DMA((2 * SUBS * nz,)),
         ],
         compiler_params=pltpu.CompilerParams(collective_id=0, has_side_effects=True, vmem_limit_bytes=40 * 2**20),
-    )(attn, w_o, w_mate, pltpu.with_memory_space_constraint(hidden, pltpu.HBM), gain)
+    )(attn, w_own, w_mate, pltpu.with_memory_space_constraint(hidden, pltpu.HBM), gain)
 
 
 def solution(mesh):
     def local_step(hidden, w_q, w_k, w_v, w_o, q_norm_w, k_norm_w, post_norm_w, k_cache, v_cache, positions):
         n_tp = mesh.shape["tp"]
-        q_rot, k_rot, v_local, posb, w_mate, k_near, v_near = project_call(
+        q_rot, k_rot, posb, w_own, w_mate, k_near, v_near = project_call(
             n_tp, hidden, w_q, w_k, w_v, w_o, q_norm_w[None, :], k_norm_w[None, :], positions, k_cache, v_cache)
-        attn, k_new, v_new = attend_call(q_rot, k_rot, v_local, posb, positions, k_near, v_near, k_cache.shape)
-        hidden_out = finish_call(n_tp, attn, w_o, w_mate, hidden, post_norm_w[None, :])
+        attn, k_new, v_new = attend_call(q_rot, k_rot, posb, k_near, v_near, k_cache.shape)
+        hidden_out = finish_call(n_tp, attn, w_own, w_mate, hidden, post_norm_w[None, :])
         return hidden_out, k_new, v_new
 
     cache_spec = P('dp', None, 'tp', None)

time: 77.4 us -> 74 us (0.956)
  Pallas kernels: 74.6 us -> 71.3 us
    pallas_call x1, Pallas kernels: 5.99 us -> 3.36 us  [attend_call(): pl.pallas_call(functools.partial(attend_kernel, slots, heads), name='atte...]
    unnamed x7 -> x3, local copies, waits for them, and re-layouts: 2.03 us -> 2.02 us
where the time goes in v5:
time: 74 us
  Pallas kernels  71.3 us (96%)
  local copies, waits for them, and re-layouts  2.02 us (3%)
    pallas_call x1, Pallas kernels, finish_call(): pl.pallas_call(functools.partial(finish_kernel, n_tp), name='finish', out...  50.1 us
    pallas_call x1, Pallas kernels, project_call(): pl.pallas_call(functools.partial(project_kernel, n_tp, slots, dim), name=...  17.8 us
    pallas_call x1, Pallas kernels, attend_call(): pl.pallas_call(functools.partial(attend_kernel, slots, heads), name='atte...  3.36 us
    unnamed x3, local copies, waits for them, and re-layouts  2.02 us

profile of v5, /device:TPU:21, one launch (start us, length us, event | category | flops | bytes accessed | tf_op | source)
XLA Modules:
  0.0 74.0 jit_solution(1527330783131266723)
XLA Ops:
  0.6 17.8 %project.1 = (bf16[512,256]{1,0:T(8,128)(2,1)S(1)}, f32[2,512,128]{2,1,0:T(8,128)S(1)}, f32[512,128]{1,0:T(8,128)S(1)}, bf16[256,4096]{1,0:T(8,128)(2,1)S(1)}, b...) custom-call(s32[4,128]{1,0:T(4,128)} %bitcast.11, ...), custom_call_target="tpu_custom_call" | custom-call | flops 3221225472 | bytes 10485760 | tf_op jit(solution)/shard_map/project/pallas_call | solution.py:183
  18.5 0.0 copy-start
  18.5 3.4 %attend.1 = (bf16[512,256]{1,0:T(8,128)(2,1)S(1)}, bf16[16384,128]{1,0:T(8,128)(2,1)}, bf16[16384,128]{1,0:T(8,128)(2,1)}) custom-call(bf16[512,256]{1,0:T(8,128)(2,1)S(1)} %get-tuple-element.13.q_ref, f32[2,512,128]{2,1,0:T(8,128)S(1)} %get-tuple-element.14.k_ref, f32[512,128]{1,0:T(8,128)S(1)} %get-tuple-element.15.posb_ref, ...), custom_call_target="tpu_custom_call" | custom-call | tf_op jit(solution)/shard_map/attend/pallas_call | solution.py:282
  21.8 0.0 copy-done
  21.9 50.1 %finish.1 = bf16[512,4096]{1,0:T(8,128)(2,1)S(1)} custom-call(bf16[512,256]{1,0:T(8,128)(2,1)S(1)} %get-tuple-element.18.o_ref, bf16[256,4096]{1,0:T(8,128)(2,1)S(1)} %get-tuple-element.19.w_ref, bf16[256,4096]{1,0:T(8,128)(2,1)S(1)} %get-tuple-element.20.w_in, bf16[512,4096]{1,0:T(8,128)(2,1)} %hid_ref.3, f32[1,4096]{1,0:T(1,128)S(1)} %bitcast.8), custom_call_target="tpu_custom_call" | custom-call | tf_op jit(solution)/shard_map/finish/pallas_call | solution.py:481
  72.0 2.0 %copy.16 = bf16[512,4096]{1,0:T(8,128)(2,1)} copy(bf16[512,4096]{1,0:T(8,128)(2,1)S(1)} %finish.1) | data formatting | bytes 8388608
Async XLA Ops:
  18.5 3.4 %copy-start = (f32[4096]{0:T(1024)S(1)}, f32[4096]{0:T(1024)}, u32[]{:S(2)}) copy-start(f32[4096]{0:T(1024)} %param.19) | copy-start | bytes 49156

commit v6 on v5

--- a/solution.py
+++ b/solution.py
@@ -15,6 +15,7 @@
 
 MESH = pl.DeviceIdType.MESH
 DEPTH_CUTS = 4
+IN_FLIGHT = 3
 TABLE_ROWS = 128
 
 
@@ -40,17 +41,17 @@
     slot_of = [(line // heads + part * (slots // 2)).astype(jnp.float32).astype(jnp.bfloat16) for part in range(2)]
 
     def insert(posb_ref, fresh_ref, start, count, old, new):
-        spots = [pl.ds(pl.multiple_of((start + r) * 2 * part_lines, 2 * part_lines) + part * part_lines, part_lines)
-                 for r in range(count) for part in range(2)]
-        before = [old[at, :] for at in spots]
+        rows = pl.ds(pl.multiple_of(start, count), count)
+        lines = pl.ds(pl.multiple_of(start * 2 * part_lines, count * 2 * part_lines), count * 2 * part_lines)
+        posb_ref, fresh_ref, old, new = posb_ref.at[rows, :], fresh_ref.at[:, rows, :], old.at[lines, :], new.at[lines, :]
         for r in range(count):
-            row = pl.ds(start + r, 1)
-            p = jnp.broadcast_to(posb_ref[row, :], (part_lines, dim)).astype(jnp.bfloat16)
-            h0 = jnp.broadcast_to(fresh_ref[0, row, :], (part_lines, dim))
-            h1 = jnp.broadcast_to(fresh_ref[1, row, :], (part_lines, dim))
+            p = jnp.broadcast_to(posb_ref[r:r + 1, :], (part_lines, dim)).astype(jnp.bfloat16)
+            h0 = jnp.broadcast_to(fresh_ref[0, r:r + 1, :], (part_lines, dim))
+            h1 = jnp.broadcast_to(fresh_ref[1, r:r + 1, :], (part_lines, dim))
             fresh = jnp.where(first, h0, h1).astype(jnp.bfloat16)
             for part in range(2):
-                new[spots[2 * r + part], :] = jnp.where(slot_of[part] == p, fresh, before[2 * r + part])
+                at = slice((2 * r + part) * part_lines, (2 * r + part + 1) * part_lines)
+                new[at, :] = jnp.where(slot_of[part] == p, fresh, old[at, :])
 
     return insert
 
@@ -77,27 +78,45 @@
             pltpu.make_async_copy(wq_ref.at[at, :], wqk.at[c, :, pl.ds(0, local)], in_sem.at[c, 1]),
             pltpu.make_async_copy(wk_ref.at[at, :], wqk.at[c, :, pl.ds(local, local)], in_sem.at[c, 2])])
     v_loads = [pltpu.make_async_copy(wv_ref.at[pl.ds(c * cut, cut), :], wv.at[c], v_sem.at[c]) for c in range(DEPTH_CUTS)]
-    for group in loads:
-        for copy in group:
-            copy.start()
     small = [pltpu.make_async_copy(src, dst, s_sem.at[i]) for i, (src, dst) in enumerate(
         ((pos_hbm, pos_ref), (table_hbm, table_ref), (qg_hbm, qg_ref), (kg_hbm, kg_ref)))]
     caches = [pltpu.make_async_copy(src, dst, c_sem.at[i]) for i, (src, dst) in enumerate(((kc_ref, kc_out), (vc_ref, vc_in), (wo_ref, wo_own)))]
-    for copy in v_loads + small + [caches[2], caches[1], caches[0]]:
-        copy.start()
-
+    queue = loads + [v_loads, small, [caches[2]], [caches[1]], [caches[0]]]
+
+    def issue(count):
+        for group in queue[:count]:
+            for copy in group:
+                copy.start()
+        del queue[:count]
+
+    issue(IN_FLIGHT)
     w_copy = pltpu.make_async_remote_copy(wo_own, wo_in, w_sem.at[0], w_sem.at[1], device_id={"tp": mate}, device_id_type=MESH)
+    lanes = e_mine.shape[1]
+    blocks = n_rows // lanes
+    def tables():
+        for copy in small:
+            copy.wait()
+        lane = lax.broadcasted_iota(jnp.int32, (lanes, TABLE_ROWS), 1)
+        which = jnp.where(lane < 3 * slots, lax.rem(lane, slots), -1).astype(jnp.float32)
+        for b in range(blocks):
+            at = slice(b * lanes, (b + 1) * lanes)
+            column = jnp.broadcast_to(pos_ref[b:b + 1, :].astype(jnp.float32), (lanes, lanes)).T
+            posb_ref[at, :] = column
+            hot = jnp.where(which == column, 1.0, 0.0).astype(jnp.bfloat16)
+            factors = jnp.dot(hot, table_ref[...], preferred_element_type=jnp.float32)
+            cosb[at, :] = factors[:, :dim]
+            sinb[at, :] = factors[:, dim:]
+
     for c in range(DEPTH_CUTS):
         for copy in loads[c]:
             copy.wait()
+        issue(1)
         part = jnp.dot(hid[c], wqk[c], preferred_element_type=jnp.float32)
         if c == 0:
             acc[...] = part
         else:
             acc[...] += part
 
-    lanes = e_mine.shape[1]
-    blocks = n_rows // lanes
     ones = jnp.ones((8, local), jnp.bfloat16)
     nt = (((1,), (1,)), ((), ()))
     for i in range(2):
@@ -109,6 +128,7 @@
                   + lax.dot_general(ones, low, nt, preferred_element_type=jnp.float32))
         for b in range(blocks):
             e_mine[i * blocks + b:i * blocks + b + 1, :] = energy[0:1, b * lanes:(b + 1) * lanes]
+    issue(len(queue))
     pl.semaphore_wait(barrier, n_tp - 1)
     sends = [pltpu.make_async_remote_copy(
         e_mine, e_in.at[off], e_send.at[off], e_recv.at[off],
@@ -117,6 +137,7 @@
         copy.start()
     caches[2].wait()
     w_copy.start()
+    tables()
 
     for c in range(DEPTH_CUTS):
         v_loads[c].wait()
@@ -126,18 +147,6 @@
                 vacc[h] = part[:, h * dim:(h + 1) * dim]
             else:
                 vacc[h] += part[:, h * dim:(h + 1) * dim]
-    for copy in small:
-        copy.wait()
-    lane = lax.broadcasted_iota(jnp.int32, (lanes, TABLE_ROWS), 1)
-    which = jnp.where(lane < 3 * slots, lax.rem(lane, slots), -1).astype(jnp.float32)
-    for b in range(blocks):
-        at = slice(b * lanes, (b + 1) * lanes)
-        column = jnp.broadcast_to(pos_ref[b:b + 1, :].astype(jnp.float32), (lanes, lanes)).T
-        posb_ref[at, :] = column
-        hot = jnp.where(which == column, 1.0, 0.0).astype(jnp.bfloat16)
-        factors = jnp.dot(hot, table_ref[...], preferred_element_type=jnp.float32)
-        cosb[at, :] = factors[:, :dim]
-        sinb[at, :] = factors[:, dim:]
     caches[1].wait()
     insert = inserter(slots, heads, dim)
 
@@ -294,7 +303,23 @@
 
 SUBS = 2
 LAG = 0
+RS_PLAN = 2
+AG_PLAN = 0
 SHARE_TILE = 2048
+
+
+def rs_plan_of(far):
+    if RS_PLAN == 0:
+        return [[(t, "L")] + ([(t + 1, "S")] if t + 1 < far else []) for t in range(far)]
+    if RS_PLAN == 1:
+        return [[(0, "L")]] + [[(t, "F")] for t in range(1, far)]
+    return [[(0, "L"), (1, "S")], [(1, "L")]] + [[(t, "F")] for t in range(2, far)]
+
+
+def ag_plan_of(far):
+    if AG_PLAN == 0:
+        return [[(t, "L")] + ([(t, "S")] if t + 1 < far else []) for t in range(far)]
+    return [[(t, "F")] for t in range(far - 1)] + [[(far - 1, "L")]]
 
 
 def finish_kernel(n_tp, o_ref, w_ref, w_in, hid_ref, gain_ref, out_ref,
@@ -352,66 +377,78 @@
         at = slice(place[j] * rows, (place[j] + 1) * rows)
         lhs_in[at, :] = o_in[pl.ds(pl.multiple_of(chunk_of(j) * rows, rows), rows), :]
 
-    def hops(d, c):
-        return far if c == long_half[d] else far - 1
-
+    def halves(d, kind):
+        return {"L": (d,), "S": (1 - d,), "F": (0, 1)}[kind]
+
+    def span(d, kind):
+        return pl.ds(0, width) if kind == "F" else pl.ds(halves(d, kind)[0] * half, half)
+
+    rs_plan, ag_plan = rs_plan_of(far), ag_plan_of(far)
     slots = {}
-    for d in range(2):
-        for c in range(2):
-            for h in range(hops(d, c)):
+    for stage_list in rs_plan:
+        for g, kind in stage_list:
+            for d in range(2):
                 for s in range(SUBS):
-                    slots[d, c, h, s] = len(slots)
-
-    def rs_message(d, c, h, s):
-        i = slots[d, c, h, s]
+                    slots[d, g, kind, s] = len(slots)
+    ag_slots = {}
+    for stage_list in ag_plan:
+        for g, kind in stage_list:
+            for d in range(2):
+                for s in range(SUBS):
+                    ag_slots[d, g, kind, s] = len(ag_slots)
+
+    def page(d, g, s):
+        return (d * far + g) * SUBS + s
+
+    def rs_message(d, g, kind, s):
+        i = slots[d, g, kind, s]
+        at = span(d, kind)
         return pltpu.make_async_remote_copy(
-            rs_out.at[i], rs_in.at[i], rs_send.at[i], rs_recv.at[i], device_id={"tp": target[d]}, device_id_type=MESH)
+            rs_out.at[page(d, g, s), :, at], rs_in.at[page(d, g, s), :, at], rs_send.at[i], rs_recv.at[i],
+            device_id={"tp": target[d]}, device_id_type=MESH)
 
     def piece(j, c, s):
         return share[place[j % nz] * rows + s * sub:place[j % nz] * rows + (s + 1) * sub, c * half:(c + 1) * half]
 
-    def rs_step(d, c, h, s):
-        ahead = hops(d, c) - h
-        j = ahead if d == 0 else -ahead
-        value = piece(j, c, s)
-        if h > 0:
-            before = rs_message(d, c, h - 1, s)
-            before.wait_recv()
-            value = value + rs_in[slots[d, c, h - 1, s]].astype(jnp.float32)
-        rs_out[slots[d, c, h, s]] = value.astype(jnp.bfloat16)
-        rs_message(d, c, h, s).start()
-
-    def ag_message(d, c, h, s):
-        j = -h if d == 0 else h
-        here = out_ref.at[pl.ds(out_row(j, s), sub), cols[c]]
-        i = slots[d, c, h, s]
+    arrived = set()
+
+    def received(d, g, c, s):
+        for kind in ("L", "S", "F"):
+            if (d, g, kind, s) in slots and c in halves(d, kind) and (d, g, kind, s) not in arrived:
+                rs_message(d, g, kind, s).wait_recv()
+                arrived.add((d, g, kind, s))
+        return rs_in[page(d, g, s), :, c * half:(c + 1) * half].astype(jnp.float32)
+
+    def rs_step(d, g, kind, s):
+        j = far - g if d == 0 else g - far
+        for c in halves(d, kind):
+            value = piece(j, c, s)
+            if g > (0 if c == d else 1):
+                value = value + received(d, g - 1, c, s)
+            rs_out[page(d, g, s), :, c * half:(c + 1) * half] = value.astype(jnp.bfloat16)
+        rs_message(d, g, kind, s).start()
+
+    def ag_message(d, g, kind, s, behind):
+        here = out_ref.at[pl.ds(out_row(-behind if d == 0 else behind, s), sub), span(d, kind)]
+        i = ag_slots[d, g, kind, s]
         return pltpu.make_async_remote_copy(
             here, here, ag_send.at[i], ag_recv.at[i], device_id={"tp": target[d]}, device_id_type=MESH)
 
-    def ag_arrival(d, c, h, s):
-        j = -(h + 1) if d == 0 else h + 1
-        here = out_ref.at[pl.ds(out_row(j, s), sub), cols[c]]
-        i = slots[d, c, h, s]
-        return pltpu.make_async_remote_copy(
-            here, here, ag_send.at[i], ag_recv.at[i], device_id={"tp": target[d]}, device_id_type=MESH)
-
     d2d = []
 
-    def d2d_start(j, c, s):
-        here = out_ref.at[pl.ds(out_row(j, s), sub), cols[c]]
+    def d2d_start(j, at, s):
+        here = out_ref.at[pl.ds(out_row(j, s), sub), at]
         i = len(d2d)
         copy = pltpu.make_async_remote_copy(here, here, d2d_send.at[i], d2d_recv.at[i], device_id={"tp": mate}, device_id_type=MESH)
         copy.start()
-        d2d.append((j, c, s))
+        d2d.append((j, at, s))
 
     def finish(s):
         total = []
         for c in range(2):
             acc = piece(0, c, s)
             for d in range(2):
-                last = hops(d, c) - 1
-                rs_message(d, c, last, s).wait_recv()
-                acc = acc + rs_in[slots[d, c, last, s]].astype(jnp.float32)
+                acc = acc + received(d, far - 1, c, s)
             share[place[0] * rows + s * sub:place[0] * rows + (s + 1) * sub, c * half:(c + 1) * half] = acc
             total.append(jnp.sum(acc * acc, axis=-1, keepdims=True))
         inv = lax.rsqrt((total[0] + total[1]) / width + NORM_EPS)
@@ -419,52 +456,51 @@
             at = slice(c * half, (c + 1) * half)
             normed = piece(0, c, s) * inv * gain_ref[:, at]
             out_ref[pl.ds(out_row(0, s), sub), at] = (hid[s * sub:(s + 1) * sub, at].astype(jnp.float32) + normed).astype(jnp.bfloat16)
-        for d in range(2):
-            for c in (long_half[d], 1 - long_half[d]):
-                ag_message(d, c, 0, s).start()
-        for c in range(2):
-            d2d_start(0, c, s)
-
-    def ag_step(h, s):
-        for c in range(2):
+        for g, kind in ag_plan[0]:
             for d in range(2):
-                if h - 1 < hops(d, c):
-                    ag_arrival(d, c, h - 1, s).wait_recv()
-                    if h < hops(d, c):
-                        ag_message(d, c, h, s).start()
-                    d2d_start(-h if d == 0 else h, c, s)
-
-    def stage(g, s):
-        if g < far:
-            for longer in (True, False):
+                ag_message(d, g, kind, s, 0).start()
+        d2d_start(0, pl.ds(0, width), s)
+
+    def ag_step(t, s):
+        for g, kind in ag_plan[t - 1]:
+            for d in range(2):
+                ag_message(d, g, kind, s, g + 1).wait_recv()
+                if t < len(ag_plan):
+                    for g_next, kind_next in ag_plan[t]:
+                        if kind_next == kind or (kind == "F" and kind_next == "L"):
+                            ag_message(d, g_next, kind_next, s, g + 1).start()
+                d2d_start(-(g + 1) if d == 0 else g + 1, span(d, kind), s)
+
+    def stage(t, s):
+        if t < far:
+            for g, kind in rs_plan[t]:
                 for d in range(2):
-                    c = long_half[d] if longer else 1 - long_half[d]
-                    if g < hops(d, c):
-                        rs_step(d, c, g, s)
-        elif g == far:
+                    rs_step(d, g, kind, s)
+        elif t == far:
             if s == 0:
                 hid_copy.wait()
             finish(s)
         else:
-            ag_step(g - far, s)
+            ag_step(t - far, s)
 
     add_shares(0, 3, lhs_in, w_in, False)
-    last_stage = 2 * far
+    last_stage = far + len(ag_plan)
     for slot in range(last_stage + 1 + LAG * (SUBS - 1)):
         if slot == 1:
             add_shares(3, nz, lhs_in, w_in, False)
         for s in range(SUBS):
-            g = slot - LAG * s
-            if 0 <= g <= last_stage:
-                stage(g, s)
+            t = slot - LAG * s
+            if 0 <= t <= last_stage:
+                stage(t, s)
 
     o_copy.wait_send()
-    for (d, c, h, s) in slots:
-        rs_message(d, c, h, s).wait_send()
-        ag_message(d, c, h, s).wait_send()
-    for i, (j, c, s) in enumerate(d2d):
-        here = out_ref.at[pl.ds(out_row(j, s), sub), cols[c]]
-        there = out_ref.at[pl.ds(pl.multiple_of((1 - k) * half_rows + chunk_of(j) * rows + s * sub, sub), sub), cols[c]]
+    for d, g, kind, s in slots:
+        rs_message(d, g, kind, s).wait_send()
+    for d, g, kind, s in ag_slots:
+        ag_message(d, g, kind, s, g).wait_send()
+    for i, (j, at, s) in enumerate(d2d):
+        here = out_ref.at[pl.ds(out_row(j, s), sub), at]
+        there = out_ref.at[pl.ds(pl.multiple_of((1 - k) * half_rows + chunk_of(j) * rows + s * sub, sub), sub), at]
         copy = pltpu.make_async_remote_copy(here, there, d2d_send.at[i], d2d_recv.at[i], device_id={"tp": mate}, device_id_type=MESH)
         copy.wait_send()
         copy.wait_recv()
@@ -490,8 +526,8 @@
             pltpu.VMEM((half_rows, depth), jnp.bfloat16),
             pltpu.VMEM((rows, width), jnp.bfloat16),
             pltpu.VMEM((half_rows, width), jnp.float32),
-            pltpu.VMEM((n_msg, sub, width // 2), jnp.bfloat16),
-            pltpu.VMEM((n_msg, sub, width // 2), jnp.bfloat16),
+            pltpu.VMEM((nz * SUBS, sub, width), jnp.bfloat16),
+            pltpu.VMEM((nz * SUBS, sub, width), jnp.bfloat16),
             pltpu.SemaphoreType.DMA,
             pltpu.SemaphoreType.DMA,
             pltpu.SemaphoreType.DMA,

time: 74 us -> 73.5 us (level)
  no operation moved by 1% of the time
where the time goes in v6:
time: 73.5 us; the launch traced here: 73.4 us
  Pallas kernels  70.7 us (96%)
  local copies, waits for them, and re-layouts  2.02 us (3%)
    pallas_call x1, Pallas kernels, finish_call(): pl.pallas_call(functools.partial(finish_kernel, n_tp), name='finish', out...  49.6 us
    pallas_call x1, Pallas kernels, project_call(): pl.pallas_call(functools.partial(project_kernel, n_tp, slots, dim), name=...  17.8 us
    pallas_call x1, Pallas kernels, attend_call(): pl.pallas_call(functools.partial(attend_kernel, slots, heads), name='atte...  3.36 us
    unnamed x3, local copies, waits for them, and re-layouts  2.02 us

profile of v6, /device:TPU:21, one launch (start us, length us, event | category | flops | bytes accessed | tf_op | source)
XLA Modules:
  0.0 73.4 jit_solution(1424702580354661248)
XLA Ops:
  0.6 17.8 %project.1 = (bf16[512,256]{1,0:T(8,128)(2,1)S(1)}, f32[2,512,128]{2,1,0:T(8,128)S(1)}, f32[512,128]{1,0:T(8,128)S(1)}, bf16[256,4096]{1,0:T(8,128)(2,1)S(1)}, b...) custom-call(s32[4,128]{1,0:T(4,128)} %bitcast.11, ...), custom_call_target="tpu_custom_call" | custom-call | flops 3221225472 | bytes 10485760 | tf_op jit(solution)/shard_map/project/pallas_call | solution.py:192
  18.5 0.0 copy-start
  18.5 3.4 %attend.1 = (bf16[512,256]{1,0:T(8,128)(2,1)S(1)}, bf16[16384,128]{1,0:T(8,128)(2,1)}, bf16[16384,128]{1,0:T(8,128)(2,1)}) custom-call(bf16[512,256]{1,0:T(8,128)(2,1)S(1)} %get-tuple-element.13.q_ref, f32[2,512,128]{2,1,0:T(8,128)S(1)} %get-tuple-element.14.k_ref, f32[512,128]{1,0:T(8,128)S(1)} %get-tuple-element.15.posb_ref, ...), custom_call_target="tpu_custom_call" | custom-call | tf_op jit(solution)/shard_map/attend/pallas_call | solution.py:291
  21.8 0.0 copy-done
  21.9 49.6 %finish.1 = bf16[512,4096]{1,0:T(8,128)(2,1)S(1)} custom-call(bf16[512,256]{1,0:T(8,128)(2,1)S(1)} %get-tuple-element.18.o_ref, bf16[256,4096]{1,0:T(8,128)(2,1)S(1)} %get-tuple-element.19.w_ref, bf16[256,4096]{1,0:T(8,128)(2,1)S(1)} %get-tuple-element.20.w_in, bf16[512,4096]{1,0:T(8,128)(2,1)} %hid_ref.3, f32[1,4096]{1,0:T(1,128)S(1)} %bitcast.8), custom_call_target="tpu_custom_call" | custom-call | tf_op jit(solution)/shard_map/finish/pallas_call | solution.py:517
  71.4 2.0 %copy.16 = bf16[512,4096]{1,0:T(8,128)(2,1)} copy(bf16[512,4096]{1,0:T(8,128)(2,1)S(1)} %finish.1) | data formatting | bytes 8388608
Async XLA Ops:
  18.5 3.4 %copy-start = (f32[4096]{0:T(1024)S(1)}, f32[4096]{0:T(1024)}, u32[]{:S(2)}) copy-start(f32[4096]{0:T(1024)} %param.19) | copy-start | bytes 49156

commit v7 on v6

--- a/solution.py
+++ b/solution.py
@@ -15,7 +15,7 @@
 
 MESH = pl.DeviceIdType.MESH
 DEPTH_CUTS = 4
-IN_FLIGHT = 3
+IN_FLIGHT = 4
 TABLE_ROWS = 128
 
 
@@ -305,7 +305,7 @@
 LAG = 0
 RS_PLAN = 2
 AG_PLAN = 0
-SHARE_TILE = 2048
+SHARE_TILE = 4096
 
 
 def rs_plan_of(far):
@@ -313,12 +313,18 @@
         return [[(t, "L")] + ([(t + 1, "S")] if t + 1 < far else []) for t in range(far)]
     if RS_PLAN == 1:
         return [[(0, "L")]] + [[(t, "F")] for t in range(1, far)]
+    if RS_PLAN == 3:
+        return [[(0, "L"), (1, "S")], [(1, "L")]] + [[(t, "F")] for t in range(2, far - 1)] + [[(far - 1, "L"), (far - 1, "S")]]
     return [[(0, "L"), (1, "S")], [(1, "L")]] + [[(t, "F")] for t in range(2, far)]
 
 
 def ag_plan_of(far):
     if AG_PLAN == 0:
         return [[(t, "L")] + ([(t, "S")] if t + 1 < far else []) for t in range(far)]
+    if AG_PLAN == 2:
+        return [[(t, "F")] if t < far - 2 else [(t, "L")] + ([(t, "S")] if t + 1 < far else []) for t in range(far)]
+    if AG_PLAN == 3:
+        return [[(t, "F")] if t < 1 else [(t, "L")] + ([(t, "S")] if t + 1 < far else []) for t in range(far)]
     return [[(t, "F")] for t in range(far - 1)] + [[(far - 1, "L")]]
 
 
@@ -355,9 +361,10 @@
 
     order = sorted(range(nz), key=lambda j: -min(j, nz - j))
     place = {j: i for i, j in enumerate(order)}
-    for j in range(nz):
-        at = slice(place[j] * rows, (place[j] + 1) * rows)
-        lhs[at, :] = o_ref[pl.ds(pl.multiple_of(k * half_rows + chunk_of(j) * rows, rows), rows), :]
+    def gather(first, last, ref, base, out):
+        for j in order[first:last]:
+            at = slice(place[j] * rows, (place[j] + 1) * rows)
+            out[at, :] = ref[pl.ds(pl.multiple_of(base + chunk_of(j) * rows, rows), rows), :]
 
     def add_shares(first, last, lhs_ref, weight, fresh):
         def one(c, carry):
@@ -371,11 +378,10 @@
 
         lax.fori_loop(0, width // SHARE_TILE, one, 0)
 
-    add_shares(0, nz, lhs, w_ref, True)
+    gather(0, nz, o_ref, k * half_rows, lhs)
+    add_shares(0, 3, lhs, w_ref, True)
     o_copy.wait_recv()
-    for j in range(nz):
-        at = slice(place[j] * rows, (place[j] + 1) * rows)
-        lhs_in[at, :] = o_in[pl.ds(pl.multiple_of(chunk_of(j) * rows, rows), rows), :]
+    gather(0, 3, o_in, 0, lhs_in)
 
     def halves(d, kind):
         return {"L": (d,), "S": (1 - d,), "F": (0, 1)}[kind]
@@ -467,7 +473,7 @@
                 ag_message(d, g, kind, s, g + 1).wait_recv()
                 if t < len(ag_plan):
                     for g_next, kind_next in ag_plan[t]:
-                        if kind_next == kind or (kind == "F" and kind_next == "L"):
+                        if set(halves(d, kind_next)) <= set(halves(d, kind)):
                             ag_message(d, g_next, kind_next, s, g + 1).start()
                 d2d_start(-(g + 1) if d == 0 else g + 1, span(d, kind), s)
 
@@ -487,6 +493,8 @@
     last_stage = far + len(ag_plan)
     for slot in range(last_stage + 1 + LAG * (SUBS - 1)):
         if slot == 1:
+            gather(3, nz, o_in, 0, lhs_in)
+            add_shares(3, nz, lhs, w_ref, True)
             add_shares(3, nz, lhs_in, w_in, False)
         for s in range(SUBS):
             t = slot - LAG * s

time: 73.5 us -> 73.1 us (level)
  no operation moved by 1% of the time
where the time goes in v7:
time: 73.1 us; the launch traced here: 73 us
  Pallas kernels  70.3 us (96%)
  local copies, waits for them, and re-layouts  2.02 us (3%)
    pallas_call x1, Pallas kernels, finish_call(): pl.pallas_call(functools.partial(finish_kernel, n_tp), name='finish', out...  49.1 us
    pallas_call x1, Pallas kernels, project_call(): pl.pallas_call(functools.partial(project_kernel, n_tp, slots, dim), name=...  17.8 us
    pallas_call x1, Pallas kernels, attend_call(): pl.pallas_call(functools.partial(attend_kernel, slots, heads), name='atte...  3.36 us
    unnamed x3, local copies, waits for them, and re-layouts  2.02 us

profile of v7, /device:TPU:21, one launch (start us, length us, event | category | flops | bytes accessed | tf_op | source)
XLA Modules:
  0.0 73.0 jit_solution(4220484903458157108)
XLA Ops:
  0.6 17.8 %project.1 = (bf16[512,256]{1,0:T(8,128)(2,1)S(1)}, f32[2,512,128]{2,1,0:T(8,128)S(1)}, f32[512,128]{1,0:T(8,128)S(1)}, bf16[256,4096]{1,0:T(8,128)(2,1)S(1)}, b...) custom-call(s32[4,128]{1,0:T(4,128)} %bitcast.11, ...), custom_call_target="tpu_custom_call" | custom-call | flops 3221225472 | bytes 10485760 | tf_op jit(solution)/shard_map/project/pallas_call | solution.py:192
  18.5 0.0 copy-start
  18.5 3.4 %attend.1 = (bf16[512,256]{1,0:T(8,128)(2,1)S(1)}, bf16[16384,128]{1,0:T(8,128)(2,1)}, bf16[16384,128]{1,0:T(8,128)(2,1)}) custom-call(bf16[512,256]{1,0:T(8,128)(2,1)S(1)} %get-tuple-element.13.q_ref, f32[2,512,128]{2,1,0:T(8,128)S(1)} %get-tuple-element.14.k_ref, f32[512,128]{1,0:T(8,128)S(1)} %get-tuple-element.15.posb_ref, ...), custom_call_target="tpu_custom_call" | custom-call | tf_op jit(solution)/shard_map/attend/pallas_call | solution.py:291
  21.8 0.0 copy-done
  21.9 49.1 %finish.1 = bf16[512,4096]{1,0:T(8,128)(2,1)S(1)} custom-call(bf16[512,256]{1,0:T(8,128)(2,1)S(1)} %get-tuple-element.18.o_ref, bf16[256,4096]{1,0:T(8,128)(2,1)S(1)} %get-tuple-element.19.w_ref, bf16[256,4096]{1,0:T(8,128)(2,1)S(1)} %get-tuple-element.20.w_in, bf16[512,4096]{1,0:T(8,128)(2,1)} %hid_ref.3, f32[1,4096]{1,0:T(1,128)S(1)} %bitcast.8), custom_call_target="tpu_custom_call" | custom-call | tf_op jit(solution)/shard_map/finish/pallas_call | solution.py:525
  71.0 2.0 %copy.16 = bf16[512,4096]{1,0:T(8,128)(2,1)} copy(bf16[512,4096]{1,0:T(8,128)(2,1)S(1)} %finish.1) | data formatting | bytes 8388608
Async XLA Ops:
  18.5 3.4 %copy-start = (f32[4096]{0:T(1024)S(1)}, f32[4096]{0:T(1024)}, u32[]{:S(2)}) copy-start(f32[4096]{0:T(1024)} %param.19) | copy-start | bytes 49156

commit v8 on v7

--- a/solution.py
+++ b/solution.py
@@ -122,7 +122,7 @@
     for i in range(2):
         rounded = acc[:, i * local:(i + 1) * local].astype(jnp.bfloat16).astype(jnp.float32)
         square = rounded * rounded
-        high = square.astype(jnp.bfloat16)
+        high = jnp.minimum(square, float(jnp.finfo(jnp.bfloat16).max)).astype(jnp.bfloat16)
         low = (square - high.astype(jnp.float32)).astype(jnp.bfloat16)
         energy = (lax.dot_general(ones, high, nt, preferred_element_type=jnp.float32)
                   + lax.dot_general(ones, low, nt, preferred_element_type=jnp.float32))
@@ -244,6 +244,7 @@
     n = lax.broadcasted_iota(jnp.int32, (heads * GROUP, wide), 1)
     own = (lax.rem(m, GROUP) == n // lines) & (m // GROUP == lax.rem(n, heads))
     slot = jnp.where(own, (lax.rem(n, lines) // heads).astype(jnp.float32), 1e9)
+    shut = jnp.where(own, -1e30, -jnp.inf)
 
     def k_copy(i):
         at = pl.ds(pl.multiple_of(i * block * lines, block * lines), block * lines)
@@ -266,7 +267,7 @@
             s = lax.dot_general(q, keys, (((1,), (1,)), ((), ())), preferred_element_type=jnp.float32) * dim ** -0.5
             at = jnp.concatenate([posb_ref[rows, :]] * heads, axis=0)
             at = jnp.concatenate([at] * (wide // at.shape[1]), axis=1)
-            scores.append(jnp.where(slot <= at, s, -1e30))
+            scores.append(jnp.where(slot <= at, s, shut))
         for g in range(n_groups):
             rows = pl.ds(pl.multiple_of(i * block + g * GROUP, GROUP), GROUP)
             values = vn_ref[pl.ds(pl.multiple_of((i * n_groups + g) * wide, wide), wide), :]

time: 73.1 us -> 73.1 us (level)
  no operation moved by 1% of the time
where the time goes in v8:
time: 73.1 us; the launch traced here: 73 us
  Pallas kernels  70.3 us (96%)
  local copies, waits for them, and re-layouts  2.02 us (3%)
    pallas_call x1, Pallas kernels, finish_call(): pl.pallas_call(functools.partial(finish_kernel, n_tp), name='finish', out...  49.1 us
    pallas_call x1, Pallas kernels, project_call(): pl.pallas_call(functools.partial(project_kernel, n_tp, slots, dim), name=...  17.8 us
    pallas_call x1, Pallas kernels, attend_call(): pl.pallas_call(functools.partial(attend_kernel, slots, heads), name='atte...  3.36 us
    unnamed x3, local copies, waits for them, and re-layouts  2.02 us

profile of v8, /device:TPU:21, one launch (start us, length us, event | category | flops | bytes accessed | tf_op | source)
XLA Modules:
  0.0 73.0 jit_solution(10425781962270279354)
XLA Ops:
  0.6 17.8 %project.1 = (bf16[512,256]{1,0:T(8,128)(2,1)S(1)}, f32[2,512,128]{2,1,0:T(8,128)S(1)}, f32[512,128]{1,0:T(8,128)S(1)}, bf16[256,4096]{1,0:T(8,128)(2,1)S(1)}, b...) custom-call(s32[4,128]{1,0:T(4,128)} %bitcast.11, ...), custom_call_target="tpu_custom_call" | custom-call | flops 3221225472 | bytes 10485760 | tf_op jit(solution)/shard_map/project/pallas_call | solution.py:192
  18.5 0.0 copy-start
  18.5 3.4 %attend.1 = (bf16[512,256]{1,0:T(8,128)(2,1)S(1)}, bf16[16384,128]{1,0:T(8,128)(2,1)}, bf16[16384,128]{1,0:T(8,128)(2,1)}) custom-call(bf16[512,256]{1,0:T(8,128)(2,1)S(1)} %get-tuple-element.13.q_ref, f32[2,512,128]{2,1,0:T(8,128)S(1)} %get-tuple-element.14.k_ref, f32[512,128]{1,0:T(8,128)S(1)} %get-tuple-element.15.posb_ref, ...), custom_call_target="tpu_custom_call" | custom-call | tf_op jit(solution)/shard_map/attend/pallas_call | solution.py:292
  21.8 0.0 copy-done
  21.9 49.1 %finish.1 = bf16[512,4096]{1,0:T(8,128)(2,1)S(1)} custom-call(bf16[512,256]{1,0:T(8,128)(2,1)S(1)} %get-tuple-element.18.o_ref, bf16[256,4096]{1,0:T(8,128)(2,1)S(1)} %get-tuple-element.19.w_ref, bf16[256,4096]{1,0:T(8,128)(2,1)S(1)} %get-tuple-element.20.w_in, bf16[512,4096]{1,0:T(8,128)(2,1)} %hid_ref.3, f32[1,4096]{1,0:T(1,128)S(1)} %bitcast.8), custom_call_target="tpu_custom_call" | custom-call | tf_op jit(solution)/shard_map/finish/pallas_call | solution.py:526
  71.0 2.0 %copy.16 = bf16[512,4096]{1,0:T(8,128)(2,1)} copy(bf16[512,4096]{1,0:T(8,128)(2,1)S(1)} %finish.1) | data formatting | bytes 8388608
Async XLA Ops:
  18.5 3.4 %copy-start = (f32[4096]{0:T(1024)S(1)}, f32[4096]{0:T(1024)}, u32[]{:S(2)}) copy-start(f32[4096]{0:T(1024)} %param.19) | copy-start | bytes 49156

commit v9 on v8

--- a/solution.py
+++ b/solution.py
@@ -304,7 +304,7 @@
 
 SUBS = 2
 LAG = 0
-RS_PLAN = 2
+RS_PLAN = 4
 AG_PLAN = 0
 SHARE_TILE = 4096
 
@@ -316,6 +316,8 @@
         return [[(0, "L")]] + [[(t, "F")] for t in range(1, far)]
     if RS_PLAN == 3:
         return [[(0, "L"), (1, "S")], [(1, "L")]] + [[(t, "F")] for t in range(2, far - 1)] + [[(far - 1, "L"), (far - 1, "S")]]
+    if RS_PLAN == 4:
+        return [[(0, "L")], [(1, "S"), (1, "L")]] + [[(t, "F")] for t in range(2, far)]
     return [[(0, "L"), (1, "S")], [(1, "L")]] + [[(t, "F")] for t in range(2, far)]
 
 

time: 73.1 us -> 72.1 us (0.986)
  Pallas kernels: 70.3 us -> 69.3 us
    pallas_call x1, Pallas kernels: 49.1 us -> 48.2 us  [finish_call(): pl.pallas_call(functools.partial(finish_kernel, n_tp), name='finish', out...]
where the time goes in v9:
time: 72.1 us; the launch traced here: 72 us
  Pallas kernels  69.3 us (96%)
  local copies, waits for them, and re-layouts  2.02 us (3%)
    pallas_call x1, Pallas kernels, finish_call(): pl.pallas_call(functools.partial(finish_kernel, n_tp), name='finish', out...  48.2 us
    pallas_call x1, Pallas kernels, project_call(): pl.pallas_call(functools.partial(project_kernel, n_tp, slots, dim), name=...  17.8 us
    pallas_call x1, Pallas kernels, attend_call(): pl.pallas_call(functools.partial(attend_kernel, slots, heads), name='atte...  3.36 us
    unnamed x3, local copies, waits for them, and re-layouts  2.02 us

profile of v9, /device:TPU:21, one launch (start us, length us, event | category | flops | bytes accessed | tf_op | source)
XLA Modules:
  0.0 72.0 jit_solution(11484840440647713376)
XLA Ops:
  0.6 17.8 %project.1 = (bf16[512,256]{1,0:T(8,128)(2,1)S(1)}, f32[2,512,128]{2,1,0:T(8,128)S(1)}, f32[512,128]{1,0:T(8,128)S(1)}, bf16[256,4096]{1,0:T(8,128)(2,1)S(1)}, b...) custom-call(s32[4,128]{1,0:T(4,128)} %bitcast.11, ...), custom_call_target="tpu_custom_call" | custom-call | flops 3221225472 | bytes 10485760 | tf_op jit(solution)/shard_map/project/pallas_call | solution.py:192
  18.5 0.0 copy-start
  18.5 3.4 %attend.1 = (bf16[512,256]{1,0:T(8,128)(2,1)S(1)}, bf16[16384,128]{1,0:T(8,128)(2,1)}, bf16[16384,128]{1,0:T(8,128)(2,1)}) custom-call(bf16[512,256]{1,0:T(8,128)(2,1)S(1)} %get-tuple-element.13.q_ref, f32[2,512,128]{2,1,0:T(8,128)S(1)} %get-tuple-element.14.k_ref, f32[512,128]{1,0:T(8,128)S(1)} %get-tuple-element.15.posb_ref, ...), custom_call_target="tpu_custom_call" | custom-call | tf_op jit(solution)/shard_map/attend/pallas_call | solution.py:292
  21.8 0.0 copy-done
  21.9 48.2 %finish.1 = bf16[512,4096]{1,0:T(8,128)(2,1)S(1)} custom-call(bf16[512,256]{1,0:T(8,128)(2,1)S(1)} %get-tuple-element.18.o_ref, bf16[256,4096]{1,0:T(8,128)(2,1)S(1)} %get-tuple-element.19.w_ref, bf16[256,4096]{1,0:T(8,128)(2,1)S(1)} %get-tuple-element.20.w_in, bf16[512,4096]{1,0:T(8,128)(2,1)} %hid_ref.3, f32[1,4096]{1,0:T(1,128)S(1)} %bitcast.8), custom_call_target="tpu_custom_call" | custom-call | tf_op jit(solution)/shard_map/finish/pallas_call | solution.py:528
  70.0 2.0 %copy.16 = bf16[512,4096]{1,0:T(8,128)(2,1)} copy(bf16[512,4096]{1,0:T(8,128)(2,1)S(1)} %finish.1) | data formatting | bytes 8388608
Async XLA Ops:
  18.5 3.4 %copy-start = (f32[4096]{0:T(1024)S(1)}, f32[4096]{0:T(1024)}, u32[]{:S(2)}) copy-start(f32[4096]{0:T(1024)} %param.19) | copy-start | bytes 49156
